TPU v7x, 512 devices: a whole 4x4x16 slice. The times are simulated.
512 devices in a mesh: seq: 64 (over z, x), img: 8 (over y, core).
Axes of the slice: x: 4, y: 4, z: 16, core: 2. Of those that a mesh axis runs over, the one named last changes fastest.
Arguments:
- inner_acts: bfloat16 [65536, 3072], P(('img', 'seq')), parts along dimension 0, may hold values from -6 to 6
- gate_acts: bfloat16 [65536, 3072], P(('img', 'seq')), parts along dimension 0, may hold values from -6 to 6
- state_proj: bfloat16 [65536, 64], P(('img', 'seq')), parts along dimension 0, may hold values from -3 to 3
- step_raw: bfloat16 [65536, 96], P(('img', 'seq')), parts along dimension 0, may hold values from -4 to 4
- conv_weight: float32 [2, 4, 3072], replicated, may hold values from -3 to 3
- conv_bias: float32 [2, 3072], replicated, may hold values from -3 to 3
- step_bias: float32 [2, 48], replicated, may hold values from -1.5 to 0.5
- decay_rate: float32 [2, 48], replicated, may hold values from 5e-06 to 0.04
- skip_gain: float32 [2, 48], replicated, may hold values from 0.5 to 2
- norm_gain: float32 [3072], replicated, may hold values from 0.5 to 1.5
Outputs:
- mixed: bfloat16 [65536, 3072], P(('img', 'seq')), parts along dimension 0
There are 8 independent parts, one for each index of `img`. A program takes and returns all parts, laid end to end along the dimension named above; an argument that names none is the same for every part. Nothing has to cross between parts.
All inputs are finite; a program needn't handle non-finite values.
Results may differ from a plain program's by a relative error of at most 0.0058.
Values may be sent and summed in bfloat16 or wider, within the bound.
A program may use at most 192 MiB of HBM per device.

v0:
```python
import jax
import jax.numpy as jnp
from jax import lax
from jax.sharding import Mesh
from jax.sharding import PartitionSpec as P

SEQ = ("seq_0", "seq_1")
IMG_SEQ = ("img", "seq_0", "seq_1")


def extended(cells, sides, width):
    for axis, dim in sides:
        count = lax.axis_size(axis)
        ends = count - 1
        head = lax.slice_in_dim(cells, 0, width, axis=dim)
        tail = lax.slice_in_dim(cells, cells.shape[dim] - width, cells.shape[dim], axis=dim)
        cells = jnp.concatenate(
            [
                lax.ppermute(tail, axis, [(i, (i + 1) % count) for i in range(ends)]),
                cells,
                lax.ppermute(head, axis, [((i + 1) % count, i) for i in range(ends)]),
            ],
            axis=dim,
        )
    return cells


def neutral_like(array, identity):
    return jax.tree.map(
        lambda a, e: jnp.broadcast_to(jnp.asarray(e, a.dtype), a.shape), array, identity
    )


def carried_in(array, axes, combine, identity, reverse):
    before = start = neutral_like(array, identity)
    running = array
    for axis in reversed(axes):
        devices, position = (lax.axis_size(axis), lax.axis_index(axis))
        pieces = jax.tree.map(lambda part: lax.all_gather(part, axis), running)
        inside, running = (start, start)
        for k in reversed(range(devices)) if reverse else range(devices):
            passed = k > position if reverse else k < position
            running = combine(running, jax.tree.map(lambda part: part[k], pieces))
            inside = jax.tree.map(lambda new, old: jnp.where(passed, new, old), running, inside)
        before = combine(inside, before)
    return before


def convolve(window, weight, bias):
    kernel = weight.shape[0]
    length = window.shape[0] - kernel + 1
    accum = jnp.zeros((length, window.shape[1]), jnp.float32) + bias[None, :]
    for offset in range(kernel):
        start = kernel - 1 - offset
        accum = accum + weight[offset][None, :] * window[start : start + length].astype(jnp.float32)
    return jax.nn.silu(accum).astype(jnp.bfloat16)


def local_terms(window, write_rows, read_rows, raw_step, weight, bias, step_bias, rate, skip):
    conved = convolve(window, weight, bias)
    length, width = conved.shape
    heads = raw_step.shape[1]
    step_size = jax.nn.softplus(raw_step.astype(jnp.float32) + step_bias[None, :])
    cumul = jnp.cumsum(-rate[None, :] * step_size, axis=0)
    later = lax.broadcasted_iota(jnp.int32, (length, length), 0)
    earlier = lax.broadcasted_iota(jnp.int32, (length, length), 1)
    causal = (later >= earlier)[None]
    spread = cumul.T[:, :, None] - cumul.T[:, None, :]
    decay = jnp.where(causal, jnp.exp(jnp.where(causal, spread, 0.0)), 0.0)
    scores = jnp.dot(read_rows, write_rows.T, preferred_element_type=jnp.float32)
    weights = (scores[None] * decay * step_size.T[:, None, :]).astype(jnp.bfloat16)
    per_head = conved.reshape(length, heads, width // heads)
    inside = jnp.einsum("hts,shp->thp", weights, per_head, preferred_element_type=jnp.float32)
    final_log = cumul[-1]
    carried = jnp.exp(final_log[None, :] - cumul) * step_size
    loaded = (carried[:, :, None] * write_rows.astype(jnp.float32)[:, None, :]).astype(jnp.bfloat16)
    end_state = jnp.einsum("shp,shn->hpn", per_head, loaded, preferred_element_type=jnp.float32)
    base = inside + skip[None, :, None] * per_head.astype(jnp.float32)
    return (base, cumul, jnp.exp(final_log), end_state)


def inter_terms(cumul, read_rows, incoming):
    readout = jnp.einsum(
        "tn,hpn->thp", read_rows.astype(jnp.float32), incoming, precision=lax.Precision.HIGHEST
    )
    return readout * jnp.exp(cumul)[:, :, None]


def combine_carry(earlier, later):
    return (earlier[0] * later[0], later[0][:, None, None] * earlier[1] + later[1])


def local(
    inner_acts,
    gate_acts,
    state_proj,
    step_raw,
    conv_weight,
    conv_bias,
    step_bias,
    decay_rate,
    skip_gain,
    norm_gain,
):
    kernel = conv_weight.shape[1]
    length, width = inner_acts.shape
    state_dim = state_proj.shape[1] // 4
    heads = step_raw.shape[1] // 2
    padded = extended(inner_acts, ((SEQ, 0),), kernel - 1)
    ahead = padded[: length + kernel - 1]
    behind = padded[::-1][: length + kernel - 1]
    flipped_proj = state_proj[::-1]
    flipped_raw = step_raw[::-1]
    forward_base, forward_log, forward_total, forward_end = local_terms(
        ahead,
        state_proj[:, 0:state_dim],
        state_proj[:, state_dim : 2 * state_dim],
        step_raw[:, :heads],
        conv_weight[0],
        conv_bias[0],
        step_bias[0],
        decay_rate[0],
        skip_gain[0],
    )
    backward_base, backward_log, backward_total, backward_end = local_terms(
        behind,
        flipped_proj[:, 2 * state_dim : 3 * state_dim],
        flipped_proj[:, 3 * state_dim : 4 * state_dim],
        flipped_raw[:, heads:],
        conv_weight[1],
        conv_bias[1],
        step_bias[1],
        decay_rate[1],
        skip_gain[1],
    )
    forward_enter = carried_in(
        (forward_total, forward_end),
        SEQ,
        combine_carry,
        (jnp.ones_like(forward_total), jnp.zeros_like(forward_end)),
        False,
    )[1]
    backward_enter = carried_in(
        (backward_total, backward_end),
        SEQ,
        combine_carry,
        (jnp.ones_like(backward_total), jnp.zeros_like(backward_end)),
        True,
    )[1]
    forward = (
        forward_base
        + inter_terms(forward_log, state_proj[:, state_dim : 2 * state_dim], forward_enter)
    ).reshape(length, width)
    backward = (
        backward_base
        + inter_terms(backward_log, flipped_proj[:, 3 * state_dim : 4 * state_dim], backward_enter)
    ).reshape(length, width)[::-1]
    gated = (forward + backward) * jax.nn.silu(gate_acts.astype(jnp.float32))
    scale = lax.rsqrt(jnp.mean(gated * gated, axis=1, keepdims=True) + 1e-05)
    return (gated * scale * norm_gain[None, :]).astype(jnp.bfloat16)


def solution(mesh):
    finer = Mesh(mesh.devices.reshape(16, 4, mesh.shape["img"]), ("seq_0", "seq_1", "img"))
    return jax.shard_map(
        local,
        mesh=finer,
        in_specs=(
            P(IMG_SEQ, None),
            P(IMG_SEQ, None),
            P(IMG_SEQ, None),
            P(IMG_SEQ, None),
            P(),
            P(),
            P(),
            P(),
            P(),
            P(),
        ),
        out_specs=P(IMG_SEQ, None),
        check_vma=False,
    )
```

profile of v0, /device:TPU:24, one launch (start us, length us, event | category | flops | bytes accessed | tf_op | source)
XLA Modules:
  0.0 275.9 jit_solution(4497553226967148044)
XLA Ops:
  6.6 0.0 all-gather.11.cloned.1.call-start
  6.6 1.6 fusion.294
  8.2 1.3 collective-permute-start.1
  9.5 1.2 constant_dynamic-update-slice_fusion.1
  10.7 0.7 fusion.295
  11.4 0.6 fusion.297
  12.0 0.1 copy.44
  12.2 0.1 copy.43
  12.3 0.1 broadcast_multiply_fusion
  12.4 0.2 reduce_window_sum.18
  12.6 0.1 exponential_multiply_fusion
  12.7 0.6 fusion.298
  13.3 11.2 %all-gather.4 = f32[4,1,48]{2,1,0:T(1,128)S(1)} all-gather(f32[1,1,48]{2,1,0:T(1,128)S(1)} %get-tuple-element.20), channel_id=1, replica_groups=mesh['seq_0'=16,'seq_1'=4,'img'=8] {'seq_1'}, dimensions={0}, use_global_device_ids=true | all-gather | bytes 960 | tf_op jit(solution)/shard_map/all_gather | solution.py:39
  24.5 0.6 broadcast_select_fusion.3
  25.1 0.6 multiply_multiply_fusion
  25.7 7.7 %slice.443 = bf16[128,3072]{1,0:T(8,128)(2,1)} reverse(bf16[128,3072]{1,0:T(8,128)(2,1)S(1)} %copy-done), dimensions={0} | reverse | bytes 1572864 | tf_op jit(solution)/shard_map/slice | solution.py:55
  33.4 0.1 copy.39
  33.4 0.1 slice.457
  33.6 1.4 fusion.293
  34.9 12.0 %slice.447 = bf16[128,3072]{1,0:T(8,128)(2,1)} reverse(bf16[128,3072]{1,0:T(8,128)(2,1)} %get-tuple-element.7), dimensions={0} | reverse | bytes 1572864 | tf_op jit(solution)/shard_map/slice | solution.py:55
  46.9 7.8 %slice.450 = bf16[128,3072]{1,0:T(8,128)(2,1)} reverse(bf16[128,3072]{1,0:T(8,128)(2,1)S(1)} %get-tuple-element.9), dimensions={0} | reverse | bytes 1572864 | tf_op jit(solution)/shard_map/slice | solution.py:55
  54.7 7.7 %slice.453 = bf16[128,3072]{1,0:T(8,128)(2,1)} reverse(bf16[128,3072]{1,0:T(8,128)(2,1)S(1)} %get-tuple-element.8), dimensions={0} | reverse | bytes 1572864 | tf_op jit(solution)/shard_map/slice | solution.py:55
  62.4 2.3 multiply_convert_fusion.5
  64.7 0.4 copy.34
  65.1 0.5 fusion.189
  65.6 15.9 %all-gather.1 = f32[192,64,16]{1,2,0:T(8,128)S(1)} all-gather(f32[48,64,16]{1,2,0:T(8,128)S(1)} %fusion.189), channel_id=3, replica_groups=mesh['seq_0'=16,'seq_1'=4,'img'=8] {'seq_1'}, dimensions={0}, use_global_device_ids=true | all-gather | bytes 983040 | tf_op jit(solution)/shard_map/all_gather | solution.py:39
  81.6 1.0 bitcast_add_fusion.2
  82.6 0.0 all-gather.11.cloned.1.call-update
  82.7 0.0 all-gather.9.cloned.1.call-start
  82.7 3.1 %collective-permute-start = (bf16[3,3072]{1,0:T(4,128)(2,1)}, bf16[3,3072]{1,0:T(4,128)(2,1)}, u32[]{:S(2)}, u32[]{:S(2)}) collective-permute-start(bf16[3,3072]{1,0:T(4,128)(2,1)} %get-tuple-element.11), channel_id=1, source_target_pairs={{0,8},{8,16},{16,24},{24,32},{32,40},{40,48},{48,56},{56,64},{64,7... | collective-permute-start | bytes 55304 | tf_op jit(solution)/shard_map/ppermute | solution.py:19
  85.8 0.2 reduce_window_sum.17
  85.9 11.1 %all-gather.2 = f32[4,1,48]{2,1,0:T(1,128)S(1)} all-gather(f32[1,1,48]{2,1,0:T(1,128)S(1)} %get-tuple-element.24), channel_id=1, replica_groups=mesh['seq_0'=16,'seq_1'=4,'img'=8] {'seq_1'}, dimensions={0}, use_global_device_ids=true | all-gather | bytes 960 | tf_op jit(solution)/shard_map/all_gather | solution.py:39
  97.1 0.6 broadcast_select_fusion.7
  97.7 1.4 exponential_multiply_fusion.1
  99.1 0.6 multiply_multiply_fusion.1
  99.6 0.9 copy.32
  100.6 2.8 %multiply_convert_fusion.6 = bf16[128,3072]{1,0:T(8,128)(2,1)} fusion(bf16[128,3072]{1,0:T(8,128)(2,1)S(1)} %copy-done, bf16[3,3072]{1,0:T(4,128)(2,1)} %collective-permute-done, f32[3072]{0:T(1024)S(1)} %bitcast.450, f32[3072]{0:T(1024)S(1)} %bitcast.451, f32[3072]{0:T(1024)S(1)} %bitcast.452, f32[3072]{0:T(1024)S(1)} %bitcast.453, f32[3072]{0:T(1024)} %bitcast.458), kind=kLoop, calls=%fused_computation.29 | loop fusion | flops 10223616 | bytes 1652736 | tf_op jit(solution)/shard_map/convert_element_type | solution.py:56
  103.4 1.5 copy.27
  105.0 0.5 fusion.188
  105.5 15.4 %all-gather = f32[192,64,16]{1,2,0:T(8,128)S(1)} all-gather(f32[48,64,16]{1,2,0:T(8,128)S(1)} %fusion.188), channel_id=2, replica_groups=mesh['seq_0'=16,'seq_1'=4,'img'=8] {'seq_1'}, dimensions={0}, use_global_device_ids=true | all-gather | bytes 983040 | tf_op jit(solution)/shard_map/all_gather | solution.py:39
  121.0 1.1 copy-done.1
  122.1 1.0 bitcast_add_fusion.6
  123.2 0.0 all-gather.9.cloned.1.call-update
  123.2 0.7 copy.38
  123.9 0.1 copy.36
  124.0 0.1 slice.455
  124.1 0.1 copy.40
  124.2 0.9 copy.31
  125.1 0.1 copy.29
  125.2 0.1 copy.33
  125.2 36.0 %all-gather.5 = f32[16,1,48]{2,1,0:T(1,128)S(1)} all-gather(f32[1,1,48]{2,1,0:T(1,128)S(1)} %copy-done.39), channel_id=1, replica_groups=mesh['seq_0'=16,'seq_1'=4,'img'=8] {'seq_0'}, dimensions={0}, use_global_device_ids=true | all-gather | bytes 3264 | tf_op jit(solution)/shard_map/all_gather | solution.py:39
  161.3 26.5 %all-gather.3 = f32[16,1,48]{2,1,0:T(1,128)S(1)} all-gather(f32[1,1,48]{2,1,0:T(1,128)S(1)} %copy-done.40), channel_id=1, replica_groups=mesh['seq_0'=16,'seq_1'=4,'img'=8] {'seq_0'}, dimensions={0}, use_global_device_ids=true | all-gather | bytes 3264 | tf_op jit(solution)/shard_map/all_gather | solution.py:39
  187.8 0.2 fusion.282
  188.0 0.2 fusion.299
  188.2 3.4 %fusion.1 = f32[48,64,128]{2,1,0:T(8,128)} fusion(bf16[128,48,64]{0,2,1:T(8,128)(2,1)S(1)} %bitcast.441, f32[48,128]{1,0:T(8,128)} %copy.38, f32[48,128]{1,0:T(8,128)S(1)} %copy.36, f32[128,128]{1,0:T(8,128)S(1)} %fusion.299, pred[128,128]{1,0:T(8,128)(4,1)S(1)} %iota_compare_fusion), kind=kOutput, calls=%fused_computation.5 | convolution fusion | flops 105381888 | bytes 2490368 | tf_op jit(solution)/shard_map/hts,shp->thp/dot_general | solution.py:73
  191.7 2.8 %fusion = f32[48,64,128]{2,1,0:T(8,128)} fusion(bf16[128,48,64]{0,2,1:T(8,128)(2,1)S(1)} %bitcast.444, f32[48,128]{1,0:T(8,128)S(1)} %copy.31, f32[48,128]{1,0:T(8,128)S(1)} %copy.29, f32[128,128]{1,0:T(8,128)S(1)} %fusion.282, pred[128,128]{1,0:T(8,128)(4,1)S(1)} %iota_compare_fusion), kind=kOutput, calls=%fused_computation.4 | convolution fusion | flops 105381888 | bytes 2490368 | tf_op jit(solution)/shard_map/hts,shp->thp/dot_general | solution.py:73
  194.5 6.3 %fusion.6 = f32[128,48,64]{0,2,1:T(8,128)} fusion(f32[48,64,128]{2,1,0:T(8,128)} %fusion.1, bf16[128,48,64]{0,2,1:T(8,128)(2,1)S(1)} %bitcast.442, f32[128,48]{0,1:T(8,128)S(1)} %copy.40, f32[48]{0:T(128)S(1)} %get-tuple-element.81, f32[16,48,64,16]{2,3,1,0:T(8,128)} %all-gather.11.cloned.1.call-done, f32[192,64,16]{1,2,0:T(8,128)S(1)} %all-gather.1, ...), kind=kOutput, calls=%fused_computation.11 | convolution fusion | flops 80412672 | bytes 7897236 | tf_op jit(solution)/shard_map/tn,hpn->thp/dot_general | solution.py:83
  200.8 1.9 copy.41
  202.7 0.7 rev.2
  203.4 54.2 %all-gather.9.cloned.1.call-done = f32[16,48,64,16]{2,3,1,0:T(8,128)} async-done(((f32[1,48,64,16]{2,3,1,0:T(8,128)}), f32[16,48,64,16]{2,3,1,0:T(8,128)}) %all-gather.9.cloned.1.call-update) | async-done | bytes 3145744 | tf_op jit(solution)/shard_map/all_gather | solution.py:39
  257.6 6.6 %fusion.7 = f32[128,48,64]{0,2,1:T(8,128)} fusion(f32[48,64,128]{2,1,0:T(8,128)} %fusion, bf16[128,48,64]{0,2,1:T(8,128)(2,1)} %bitcast.445, f32[128,48]{0,1:T(8,128)S(1)} %copy.33, f32[48]{0:T(128)S(1)} %get-tuple-element.82, f32[16,48,64,16]{2,3,1,0:T(8,128)} %all-gather.9.cloned.1.call-done, f32[192,64,16]{1,2,0:T(8,128)} %copy-done.1, ...), kind=kOutput, calls=%fused_computation.14 | convolution fusion | flops 80412672 | bytes 7904276 | tf_op jit(solution)/shard_map/tn,hpn->thp/dot_general | solution.py:83
  264.2 1.9 copy.42
  266.1 1.8 multiply_reduce_fusion
  267.9 1.1 multiply_convert_fusion.4
  (107 shorter events, 0.3 us)
Async XLA Ops:
  6.5 19.1 %copy-start = (bf16[128,3072]{1,0:T(8,128)(2,1)S(1)}, bf16[128,3072]{1,0:T(8,128)(2,1)}, u32[]{:S(2)}) copy-start(bf16[128,3072]{1,0:T(8,128)(2,1)} %param.10) | copy-start | bytes 2359300
  6.5 4.1 %copy-start.5 = (f32[2,4,3072]{2,1,0:T(4,128)S(1)}, f32[2,4,3072]{2,1,0:T(4,128)}, u32[]{:S(2)}) copy-start(f32[2,4,3072]{2,1,0:T(4,128)} %param.14) | copy-start | bytes 294916
  6.5 4.8 %copy-start.18 = (f32[2,3072]{1,0:T(2,128)S(1)}, f32[2,3072]{1,0:T(2,128)}, u32[]{:S(2)}) copy-start(f32[2,3072]{1,0:T(2,128)} %param.15) | copy-start | bytes 73732
  6.5 5.5 %copy-start.19 = (bf16[128,96]{0,1:T(8,128)(2,1)S(1)}, bf16[128,96]{0,1:T(8,128)(2,1)}, u32[]{:S(2)}) copy-start(bf16[128,96]{0,1:T(8,128)(2,1)} %param.13) | copy-start | bytes 73732
  6.5 5.7 %copy-start.41 = (f32[2,48]{1,0:T(2,128)S(1)}, f32[2,48]{1,0:T(2,128)}, u32[]{:S(2)}) copy-start(f32[2,48]{1,0:T(2,128)} %param.16) | copy-start | bytes 1156
  6.5 5.8 %copy-start.42 = (f32[2,48]{1,0:T(2,128)S(1)}, f32[2,48]{1,0:T(2,128)}, u32[]{:S(2)}) copy-start(f32[2,48]{1,0:T(2,128)} %param.17) | copy-start | bytes 1156
  6.6 6.1 %copy-start.16 = (bf16[128,64]{0,1:T(8,128)(2,1)S(1)}, bf16[128,64]{0,1:T(8,128)(2,1)}, u32[]{:S(2)}) copy-start(bf16[128,64]{0,1:T(8,128)(2,1)} %param.12) | copy-start | bytes 49156
  6.6 187.9 %all-gather.11.cloned.1.call-start = ((), (), s32[]{:S(2)}) async-start(), calls=%async_computation.1 | async-start | bytes 6684672 | tf_op jit(solution)/shard_map/all_gather | solution.py:39
  8.2 25.4 %collective-permute-start.1 = (bf16[3,3072]{1,0:T(4,128)(2,1)S(1)}, bf16[3,3072]{1,0:T(4,128)(2,1)S(1)}, u32[]{:S(2)}, u32[]{:S(2)}) collective-permute-start(bf16[3,3072]{1,0:T(4,128)(2,1)S(1)} %get-tuple-element.10), channel_id=1, source_target_pairs={{8,0},{16,8},{24,16},{32,24},{40,32},{48,40},{56,48},{64,56},{72,6... | collective-permute-start | bytes 55304 | tf_op jit(solution)/shard_map/ppermute | solution.py:21
  12.3 1.0 copy-start.22
  33.5 1.4 copy-start.13
  46.9 15.4 %copy-start.3 = (bf16[128,3072]{1,0:T(8,128)(2,1)S(1)}, bf16[128,3072]{1,0:T(8,128)(2,1)}, u32[]{:S(2)}) copy-start(bf16[128,3072]{1,0:T(8,128)(2,1)} %slice.443) | copy-start | bytes 2359300
  46.9 15.4 %copy-start.10 = (f32[1,1,3072]{2,1,0:T(1,128)S(1)}, f32[1,1,3072]{2,1,0:T(1,128)}, u32[]{:S(2)}) copy-start(f32[1,1,3072]{2,1,0:T(1,128)} %get-tuple-element.18) | copy-start | bytes 36868
  46.9 15.4 %copy-start.11 = (f32[1,1,3072]{2,1,0:T(1,128)S(1)}, f32[1,1,3072]{2,1,0:T(1,128)}, u32[]{:S(2)}) copy-start(f32[1,1,3072]{2,1,0:T(1,128)} %get-tuple-element.19) | copy-start | bytes 36868
  46.9 15.5 %copy-start.12 = (f32[1,3072]{1,0:T(1,128)S(1)}, f32[1,3072]{1,0:T(1,128)}, u32[]{:S(2)}) copy-start(f32[1,3072]{1,0:T(1,128)} %get-tuple-element.32) | copy-start | bytes 36868
  54.7 7.7 %copy-start.4 = (bf16[128,3072]{1,0:T(8,128)(2,1)S(1)}, bf16[128,3072]{1,0:T(8,128)(2,1)}, u32[]{:S(2)}) copy-start(bf16[128,3072]{1,0:T(8,128)(2,1)} %slice.447) | copy-start | bytes 2359300
  65.0 16.5 %copy-start.23 = (f32[48]{0:T(128)S(1)}, f32[48]{0:T(128)}, u32[]{:S(2)}) copy-start(f32[48]{0:T(128)} %get-tuple-element.70) | copy-start | bytes 580
  65.1 16.5 %copy-start.27 = (f32[48]{0:T(128)S(1)}, f32[48]{0:T(128)}, u32[]{:S(2)}) copy-start(f32[48]{0:T(128)} %get-tuple-element.72) | copy-start | bytes 580
  65.1 16.5 %copy-start.29 = (f32[48]{0:T(128)S(1)}, f32[48]{0:T(128)}, u32[]{:S(2)}) copy-start(f32[48]{0:T(128)} %get-tuple-element.73) | copy-start | bytes 580
  65.1 16.5 %copy-start.31 = (f32[48]{0:T(128)S(1)}, f32[48]{0:T(128)}, u32[]{:S(2)}) copy-start(f32[48]{0:T(128)} %get-tuple-element.74) | copy-start | bytes 580
  81.6 19.0 %copy-start.6 = (f32[1,1,3072]{2,1,0:T(1,128)S(1)}, f32[1,1,3072]{2,1,0:T(1,128)}, u32[]{:S(2)}) copy-start(f32[1,1,3072]{2,1,0:T(1,128)} %get-tuple-element.14) | copy-start | bytes 36868
  81.6 19.0 %copy-start.7 = (f32[1,1,3072]{2,1,0:T(1,128)S(1)}, f32[1,1,3072]{2,1,0:T(1,128)}, u32[]{:S(2)}) copy-start(f32[1,1,3072]{2,1,0:T(1,128)} %get-tuple-element.15) | copy-start | bytes 36868
  81.6 19.0 %copy-start.8 = (f32[1,1,3072]{2,1,0:T(1,128)S(1)}, f32[1,1,3072]{2,1,0:T(1,128)}, u32[]{:S(2)}) copy-start(f32[1,1,3072]{2,1,0:T(1,128)} %get-tuple-element.16) | copy-start | bytes 36868
  81.6 19.0 %copy-start.9 = (f32[1,1,3072]{2,1,0:T(1,128)S(1)}, f32[1,1,3072]{2,1,0:T(1,128)}, u32[]{:S(2)}) copy-start(f32[1,1,3072]{2,1,0:T(1,128)} %get-tuple-element.17) | copy-start | bytes 36868
  82.7 174.9 %all-gather.9.cloned.1.call-start = ((), (), s32[]{:S(2)}) async-start(), calls=%async_computation | async-start | bytes 6684672 | tf_op jit(solution)/shard_map/all_gather | solution.py:39
  82.7 17.8 %collective-permute-start = (bf16[3,3072]{1,0:T(4,128)(2,1)}, bf16[3,3072]{1,0:T(4,128)(2,1)}, u32[]{:S(2)}, u32[]{:S(2)}) collective-permute-start(bf16[3,3072]{1,0:T(4,128)(2,1)} %get-tuple-element.11), channel_id=1, source_target_pairs={{0,8},{8,16},{16,24},{24,32},{32,40},{40,48},{48,56},{56,64},{64,7... | collective-permute-start | bytes 55304 | tf_op jit(solution)/shard_map/ppermute | solution.py:19
  100.6 4.4 %copy-start.15 = (f32[128,16]{0,1:T(8,128)S(1)}, f32[128,16]{0,1:T(8,128)}, u32[]{:S(2)}) copy-start(f32[128,16]{0,1:T(8,128)} %get-tuple-element.35) | copy-start | bytes 24580
  105.0 86.7 %copy-start.2 = (bf16[128,3072]{0,1:T(8,128)(2,1)}, bf16[128,3072]{0,1:T(8,128)(2,1)S(1)}, u32[]{:S(2)}) copy-start(bf16[128,3072]{0,1:T(8,128)(2,1)S(1)} %copy.27) | copy-start | bytes 2359300
  105.0 17.1 %copy-start.25 = (f32[48]{0:T(128)S(1)}, f32[48]{0:T(128)}, u32[]{:S(2)}) copy-start(f32[48]{0:T(128)} %get-tuple-element.76) | copy-start | bytes 580
  105.0 17.1 %copy-start.33 = (f32[48]{0:T(128)S(1)}, f32[48]{0:T(128)}, u32[]{:S(2)}) copy-start(f32[48]{0:T(128)} %get-tuple-element.78) | copy-start | bytes 580
  105.0 17.1 %copy-start.35 = (f32[48]{0:T(128)S(1)}, f32[48]{0:T(128)}, u32[]{:S(2)}) copy-start(f32[48]{0:T(128)} %get-tuple-element.79) | copy-start | bytes 580
  105.0 17.1 %copy-start.37 = (f32[48]{0:T(128)S(1)}, f32[48]{0:T(128)}, u32[]{:S(2)}) copy-start(f32[48]{0:T(128)} %get-tuple-element.80) | copy-start | bytes 580
  120.9 1.2 copy-start.1
  120.9 3.0 %copy-start.20 = (bf16[128,16]{0,1:T(8,128)(2,1)S(1)}, bf16[128,16]{0,1:T(8,128)(2,1)}, u32[]{:S(2)}) copy-start(bf16[128,16]{0,1:T(8,128)(2,1)} %get-tuple-element.36) | copy-start | bytes 12292
  121.0 4.3 %copy-start.39 = (f32[1,1,48]{2,1,0:T(1,128)S(1)}, f32[1,1,48]{2,1,0:T(1,128)}, u32[]{:S(2)}) copy-start(f32[1,1,48]{2,1,0:T(1,128)} %get-tuple-element.71) | copy-start | bytes 580
  121.0 40.3 %copy-start.40 = (f32[1,1,48]{2,1,0:T(1,128)S(1)}, f32[1,1,48]{2,1,0:T(1,128)}, u32[]{:S(2)}) copy-start(f32[1,1,48]{2,1,0:T(1,128)} %get-tuple-element.77) | copy-start | bytes 580
  121.0 66.8 %copy-start.43 = (f32[2,48]{1,0:T(2,128)S(1)}, f32[2,48]{1,0:T(2,128)}, u32[]{:S(2)}) copy-start(f32[2,48]{1,0:T(2,128)} %param.18) | copy-start | bytes 1156
  121.0 66.9 %copy-start.17 = (bf16[128,64]{0,1:T(8,128)(2,1)S(1)}, bf16[128,64]{0,1:T(8,128)(2,1)}, u32[]{:S(2)}) copy-start(bf16[128,64]{0,1:T(8,128)(2,1)} %param.12) | copy-start | bytes 49156
  121.0 67.0 %copy-start.14 = (bf16[128,16]{0,1:T(8,128)(2,1)S(1)}, bf16[128,16]{0,1:T(8,128)(2,1)}, u32[]{:S(2)}) copy-start(bf16[128,16]{0,1:T(8,128)(2,1)} %copy-done.13) | copy-start | bytes 12292
  191.6 2.8 %copy-start.24 = (f32[48]{0:T(128)S(1)}, f32[48]{0:T(128)}, u32[]{:S(2)}) copy-start(f32[48]{0:T(128)} %get-tuple-element.70) | copy-start | bytes 580
  191.6 2.8 %copy-start.28 = (f32[48]{0:T(128)S(1)}, f32[48]{0:T(128)}, u32[]{:S(2)}) copy-start(f32[48]{0:T(128)} %get-tuple-element.72) | copy-start | bytes 580
  191.6 2.8 %copy-start.30 = (f32[48]{0:T(128)S(1)}, f32[48]{0:T(128)}, u32[]{:S(2)}) copy-start(f32[48]{0:T(128)} %get-tuple-element.73) | copy-start | bytes 580
  191.6 2.8 %copy-start.32 = (f32[48]{0:T(128)S(1)}, f32[48]{0:T(128)}, u32[]{:S(2)}) copy-start(f32[48]{0:T(128)} %get-tuple-element.74) | copy-start | bytes 580
  191.7 2.8 %copy-start.44 = (f32[48]{0:T(128)S(1)}, f32[48]{0:T(128)}, u32[]{:S(2)}) copy-start(f32[48]{0:T(128)} %get-tuple-element.69) | copy-start | bytes 580
  202.7 54.9 %copy-start.26 = (f32[48]{0:T(128)S(1)}, f32[48]{0:T(128)}, u32[]{:S(2)}) copy-start(f32[48]{0:T(128)} %get-tuple-element.76) | copy-start | bytes 580
  202.7 54.9 %copy-start.34 = (f32[48]{0:T(128)S(1)}, f32[48]{0:T(128)}, u32[]{:S(2)}) copy-start(f32[48]{0:T(128)} %get-tuple-element.78) | copy-start | bytes 580
  202.7 54.9 %copy-start.36 = (f32[48]{0:T(128)S(1)}, f32[48]{0:T(128)}, u32[]{:S(2)}) copy-start(f32[48]{0:T(128)} %get-tuple-element.79) | copy-start | bytes 580
  202.7 54.9 %copy-start.38 = (f32[48]{0:T(128)S(1)}, f32[48]{0:T(128)}, u32[]{:S(2)}) copy-start(f32[48]{0:T(128)} %get-tuple-element.80) | copy-start | bytes 580
  202.7 54.9 %copy-start.45 = (f32[48]{0:T(128)S(1)}, f32[48]{0:T(128)}, u32[]{:S(2)}) copy-start(f32[48]{0:T(128)} %get-tuple-element.75) | copy-start | bytes 580
  266.1 1.8 copy-start.21
Sparse Core Ops, SparseCore 0:
  82.8 89.8 all-gather.10
  174.7 82.8 all-gather.8
where the time goes:
time: 278 us; the launch traced here: 276 us
  blocking collectives  116 us (42%)
  waiting for transfers between devices  54.2 us (19%)
  local copies, waits for them, and re-layouts  51.5 us (19%)
  matrix products  20.5 us (7%)
  other arithmetic  15 us (5%)
  between operations  14.1 us (5%)
  starting transfers between devices  4.41 us (2%)
    all_gather x6, blocking collectives, carried_in(): pieces = jax.tree.map(lambda part: lax.all_gather(part, axis), running)  116 us
    all_gather x2, waiting for transfers between devices, carried_in(): pieces = jax.tree.map(lambda part: lax.all_gather(part, axis), running)  54.2 us
    slice x5, local copies, waits for them, and re-layouts, convolve(): window[start:start + length].astype(jnp.float32)  36.5 us
    dot_general x2, matrix products, inter_terms(): jnp.einsum('tn,hpn->thp', read_rows.astype(jnp.float32), incoming, precis...  13 us
    dot_general x2, matrix products, local_terms(): jnp.einsum('hts,shp->thp', weights, per_head, preferred_element_type=jnp....  6.18 us
  transfers between devices with their start and end apart: 4, of which 1 were waited for; matrix products, arithmetic and copies ran while one was open for 14% of the time, Pallas kernels for 0%

commit v1 on v0

v1 whole, which is shorter than its diff:
```python
import functools

import jax
import jax.numpy as jnp
from jax import lax
from jax.experimental import pallas as pl
from jax.experimental.pallas import tpu as pltpu
from jax.sharding import PartitionSpec as P

MESH = pl.DeviceIdType.MESH
F32 = jnp.float32
BF16 = jnp.bfloat16
LANES = 128
HEAD = 64
GROUP = 8


def split(v):
    high = v.astype(BF16).astype(F32)
    return jnp.concatenate([high, v - high], axis=1).astype(BF16)


def spreader(block, heads, rows):
    row = lax.broadcasted_iota(jnp.int32, (rows, LANES), 0)
    lane = lax.broadcasted_iota(jnp.int32, (rows, LANES), 1)
    row = jnp.where(row >= heads, row - heads, row)
    head = 2 * block + jnp.where(lane >= HEAD, 1, 0)
    return jnp.where(row == head, 1.0, 0.0).astype(BF16)


def dot(a, b):
    return jnp.dot(a, b, preferred_element_type=F32)


def silu(v):
    half = 0.5 * v
    return half + half * jnp.tanh(half)


def kernel(
    n, group, heads, kernel_taps,
    x_hbm, gate_hbm, proj_hbm, raw_hbm, cw_hbm, cb_hbm, sb_hbm, rate_hbm, skip_hbm, gain_hbm,
    out_hbm,
    xb, gb, ob, xs, cf, cr, gf, gr, u, ef, er,
    proj_v, raw_v, cw_v, cb_v, sb_v, rate_v, skip_v, gain_v,
    lhs_g, lhs_e, lhs_x, mf, mr, bt, cm,
    prev_v, next_v, tot_v, tots_v, totg_v, totr_v,
    send1, recv1, send2, recv2, send3, recv3, sumsq,
    x_sem, g_sem, o_sem, s_sem, h_send, h_recv,
    t1_send, t1_recv, t2_send, t2_recv, c1_send, c1_recv, c2_send, c2_recv, c3_send, c3_recv,
):
    rows = xb.shape[1]
    blocks = xb.shape[0]
    per = blocks // group
    groups = n // group
    states = bt.shape[1]
    me = lax.axis_index("seq")
    mem = lax.rem(me, group)
    grp = lax.div(me, group)
    base = me - mem

    def lanes(j):
        return pl.ds(pl.multiple_of(j * LANES, LANES), LANES)

    def member(r):
        return lax.rem(mem + r, group)

    def far(r):
        return lax.rem(grp + r, groups)

    small = [
        (raw_hbm, raw_v), (sb_hbm, sb_v), (rate_hbm, rate_v), (proj_hbm, proj_v),
        (skip_hbm, skip_v), (cw_hbm, cw_v), (cb_hbm, cb_v), (gain_hbm, gain_v),
    ]
    loads = [pltpu.make_async_copy(a, b, s_sem.at[i]) for i, (a, b) in enumerate(small)]
    for copy in loads:
        copy.start()

    def x_copy(j):
        return pltpu.make_async_copy(x_hbm.at[:, lanes(j)], xb.at[j], x_sem.at[j])

    def g_copy(j):
        return pltpu.make_async_copy(gate_hbm.at[:, lanes(j)], gb.at[j], g_sem.at[j])

    def o_copy(j):
        return pltpu.make_async_copy(ob.at[j], out_hbm.at[:, lanes(j)], o_sem.at[j])

    def start_x(j, carry):
        x_copy(j).start()
        return carry

    lax.fori_loop(0, blocks, start_x, 0)

    barrier = pltpu.get_barrier_semaphore()
    after = lax.rem(me + 1, n)
    before = lax.rem(me + n - 1, n)
    for peer in (after, before):
        pl.semaphore_signal(barrier, inc=1, device_id={"seq": peer}, device_id_type=MESH)

    def greet_group(r, carry):
        pl.semaphore_signal(
            barrier, inc=1, device_id={"seq": base + member(r)}, device_id_type=MESH
        )
        return carry

    def greet_far(r, carry):
        pl.semaphore_signal(
            barrier, inc=1, device_id={"seq": far(r) * group + mem}, device_id_type=MESH
        )
        return carry

    lax.fori_loop(1, groups, greet_far, 0)
    lax.fori_loop(1, group, greet_group, 0)

    def start_g(j, carry):
        g_copy(j).start()
        return carry

    lax.fori_loop(0, blocks, start_g, 0)
    for copy in loads:
        copy.wait()

    later = lax.broadcasted_iota(jnp.int32, (rows, rows), 0)
    earlier = lax.broadcasted_iota(jnp.int32, (rows, rows), 1)
    masks = (later >= earlier, later <= earlier)
    lasts = (rows - 1, 0)
    raw = raw_v[...].astype(F32)
    proj = proj_v[...].astype(F32)
    proj_t = proj.T
    zeros = jnp.zeros((16 - 2, heads), F32)
    grow, decay, total, skips = [], [], [], []
    for d in range(2):
        v = raw[:, d * heads : (d + 1) * heads] + sb_v[d : d + 1, :]
        step = jnp.maximum(v, 0.0) + jnp.log1p(jnp.exp(-jnp.abs(v)))
        tri = jnp.where(masks[d], 1.0, 0.0)
        cumul = jnp.dot(
            tri, -rate_v[d : d + 1, :] * step, precision=lax.Precision.HIGHEST,
            preferred_element_type=F32,
        )
        grow.append(jnp.exp(-cumul) * step)
        decay.append(jnp.exp(cumul))
        total.append(jnp.exp(cumul[lasts[d] : lasts[d] + 1, :]))
        skips.append(skip_v[d : d + 1, :])
        first = 2 * d * states
        write_t = proj_t[first : first + states, :].astype(BF16)
        read = proj[:, first + states : first + 2 * states].astype(BF16)
        bt[d] = write_t
        cm[d] = read
        scores = jnp.where(masks[d], dot(read, write_t), 0.0).astype(BF16)
        (mf, mr)[d][...] = scores
    lhs_g[...] = split(jnp.concatenate(grow, axis=0))
    lhs_e[...] = split(jnp.concatenate(decay + skips + [zeros], axis=0))
    lhs_x[...] = split(
        jnp.concatenate([grow[0][:16], grow[1][rows - 16 :]] + total + [zeros], axis=0)
    )
    tot_v[...] = jnp.concatenate(
        [
            jnp.concatenate(total + [jnp.zeros((6, heads), F32)], axis=0),
            jnp.zeros((8, LANES - heads), F32),
        ],
        axis=1,
    )

    def taps(d, j, first, count):
        acc = jnp.zeros((count, LANES), F32) + cb_v[d : d + 1, lanes(j)]
        for k in range(kernel_taps):
            shift = -k if d == 0 else k
            acc = acc + cw_v[d, k : k + 1, lanes(j)] * xs[j, pl.ds(8 + first + shift, count), :]
        return silu(acc).astype(BF16)

    def conv(j, carry):
        x_copy(j).wait()
        xs[j, pl.ds(0, 8), :] = jnp.zeros((8, LANES), F32)
        xs[j, pl.ds(8 + rows, 8), :] = jnp.zeros((8, LANES), F32)
        xs[j, pl.ds(8, rows), :] = xb[j].astype(F32)
        wide = dot(lhs_g[...], spreader(j, heads, 2 * heads))
        for d in range(2):
            conved = taps(d, j, 0, rows)
            (cf, cr)[d][j] = conved
            scaled = wide[d * rows : (d + 1) * rows] * conved.astype(F32)
            (gf, gr)[d][j] = scaled.astype(BF16)
        return carry

    lax.fori_loop(0, blocks, conv, 0)

    pl.semaphore_wait(barrier, 2 + (groups - 1) + (group - 1))
    edge = 8
    halo = [
        pltpu.make_async_remote_copy(
            src_ref=x_hbm.at[pl.ds(rows - edge, edge)], dst_ref=prev_v,
            send_sem=h_send.at[0], recv_sem=h_recv.at[0],
            device_id={"seq": after}, device_id_type=MESH,
        ),
        pltpu.make_async_remote_copy(
            src_ref=x_hbm.at[pl.ds(0, edge)], dst_ref=next_v,
            send_sem=h_send.at[1], recv_sem=h_recv.at[1],
            device_id={"seq": before}, device_id_type=MESH,
        ),
    ]
    for copy in halo:
        copy.start()

    def near_copy(src, dst, ss, rs, r):
        return pltpu.make_async_remote_copy(
            src_ref=src, dst_ref=dst, send_sem=ss.at[r - 1], recv_sem=rs.at[r - 1],
            device_id={"seq": base + member(r)}, device_id_type=MESH,
        )

    def far_copy(src, dst, ss, rs, r):
        return pltpu.make_async_remote_copy(
            src_ref=src, dst_ref=dst, send_sem=ss.at[r - 1], recv_sem=rs.at[r - 1],
            device_id={"seq": far(r) * group + mem}, device_id_type=MESH,
        )

    def t1(r):
        return near_copy(tot_v, tots_v.at[mem], t1_send, t1_recv, r)

    def t2(r):
        return far_copy(totg_v, totr_v.at[grp], t2_send, t2_recv, r)

    def c1(r):
        return near_copy(send1.at[member(r)], recv1.at[mem], c1_send, c1_recv, r)

    def c2(r):
        ahead = jnp.where(far(r) > grp, 0, 1)
        return far_copy(send2.at[ahead], recv2.at[grp], c2_send, c2_recv, r)

    def c3(r):
        return near_copy(send3.at[member(r)], recv3.at[mem], c3_send, c3_recv, r)

    def loop(first, last, action):
        def body(r, carry):
            action(r)
            return carry

        lax.fori_loop(first, last, body, 0)

    loop(1, group, lambda r: t1(r).start())
    tots_v[mem] = tot_v[...]

    for copy in halo:
        copy.wait()
    loop(1, group, lambda r: t1(r).wait())

    def edges(j, carry):
        has_before = jnp.where(me > 0, 1.0, 0.0)
        has_after = jnp.where(me < n - 1, 1.0, 0.0)
        xs[j, pl.ds(0, 8), :] = prev_v[:, lanes(j)].astype(F32) * has_before
        xs[j, pl.ds(8 + rows, 8), :] = next_v[:, lanes(j)].astype(F32) * has_after
        return carry

    lax.fori_loop(0, blocks, edges, 0)

    def finish(j, place, buffer):
        wide = dot(lhs_x[...], spreader(j, heads, 2 * heads))
        ends = []
        for d in range(2):
            first = (0, rows - 16)[d]
            conved = taps(d, j, first, 16)
            (cf, cr)[d][j, pl.ds(first, 16), :] = conved
            scaled = wide[d * 16 : (d + 1) * 16] * conved.astype(F32)
            (gf, gr)[d][j, pl.ds(first, 16), :] = scaled.astype(BF16)
            end = dot(bt[d], (gf, gr)[d][j]) * wide[32 + d : 33 + d]
            ends.append(end)
        buffer[place] = jnp.concatenate(ends, axis=0).astype(BF16)

    def ends(r):
        owner = member(r)
        for b in range(per):
            finish(owner * per + b, (owner, b), send1)
        c1(r).start()

    loop(1, group, ends)
    for b in range(per):
        finish(mem * per + b, (mem, b), recv1)

    product = tots_v[0]
    for m in range(1, group):
        product = product * tots_v[m]
    totg_v[...] = product
    loop(1, groups, lambda r: t2(r).start())
    totr_v[grp] = product

    def inner(j, carry):
        g_copy(j).wait()
        wide = dot(lhs_e[...], spreader(j, heads, 2 * heads))
        gate = silu(gb[j].astype(F32))
        far_f, far_r = wide[:rows] * gate, wide[rows : 2 * rows] * gate
        ef[j] = far_f
        er[j] = far_r
        direct = (
            wide[2 * rows : 2 * rows + 1] * cf[j].astype(F32)
            + wide[2 * rows + 1 : 2 * rows + 2] * cr[j].astype(F32)
        )
        u[j] = (
            direct * gate + far_f * dot(mf[...], gf[j]) + far_r * dot(mr[...], gr[j])
        )
        return carry

    lax.fori_loop(0, blocks, inner, 0)

    loop(1, group, lambda r: c1(r).wait_recv())

    def spread(values, b):
        flat = values[...].reshape(-1, LANES)
        high = flat.astype(BF16)
        low = (flat - high.astype(F32)).astype(BF16)
        ones = spreader(mem * per + b, LANES, LANES)
        return dot(high, ones) + dot(low, ones)

    near_t = [spread(tots_v, b) for b in range(per)]

    def part(ref, m, b, d):
        return ref[m, b, pl.ds(d * states, states), :].astype(F32)

    for b in range(per):
        run_f = jnp.zeros((states, LANES), F32)
        run_r = jnp.zeros((states, LANES), F32)
        for m in range(group):
            run_f = run_f * near_t[b][8 * m : 8 * m + 1] + part(recv1, m, b, 0)
            k = group - 1 - m
            run_r = run_r * near_t[b][8 * k + 1 : 8 * k + 2] + part(recv1, k, b, 1)
        send2[0, b] = run_f.astype(BF16)
        send2[1, b] = run_r.astype(BF16)
    loop(1, groups, lambda r: c2(r).start())
    loop(1, groups, lambda r: t2(r).wait())
    far_t = [spread(totr_v, b) for b in range(per)]
    recv2[grp] = send2[0]
    loop(1, groups, lambda r: c2(r).wait_recv())

    for b in range(per):
        run_f = jnp.zeros((states, LANES), F32)
        run_r = jnp.zeros((states, LANES), F32)
        for g in range(groups):
            new = run_f * far_t[b][8 * g : 8 * g + 1] + recv2[g, b].astype(F32)
            run_f = jnp.where(g < grp, new, run_f)
            k = groups - 1 - g
            new = run_r * far_t[b][8 * k + 1 : 8 * k + 2] + recv2[k, b].astype(F32)
            run_r = jnp.where(k > grp, new, run_r)
        for m in range(group):
            send3[m, b, pl.ds(0, states), :] = run_f.astype(BF16)
            run_f = run_f * near_t[b][8 * m : 8 * m + 1] + part(recv1, m, b, 0)
            k = group - 1 - m
            send3[k, b, pl.ds(states, states), :] = run_r.astype(BF16)
            run_r = run_r * near_t[b][8 * k + 1 : 8 * k + 2] + part(recv1, k, b, 1)
    loop(1, group, lambda r: c3(r).start())
    recv3[mem] = send3[mem]

    sumsq[...] = jnp.zeros_like(sumsq)

    def outer(owner):
        for b in range(per):
            j = owner * per + b
            gated = (
                u[j]
                + ef[j] * dot(cm[0], recv3[owner, b, pl.ds(0, states), :])
                + er[j] * dot(cm[1], recv3[owner, b, pl.ds(states, states), :])
            )
            u[j] = gated
            sumsq[...] += gated * gated

    outer(mem)

    def arrived(r):
        c3(r).wait_recv()
        outer(lax.rem(mem + group - r, group))

    loop(1, group, arrived)
    mean = jnp.sum(sumsq[...], axis=1, keepdims=True) * (1.0 / (blocks * LANES))
    scale = lax.rsqrt(mean + 1e-05)

    def write(j, carry):
        ob[j] = (u[j] * scale * gain_v[:, lanes(j)]).astype(BF16)
        o_copy(j).start()
        return carry

    lax.fori_loop(0, blocks, write, 0)
    loop(1, group, lambda r: c1(r).wait_send())
    loop(1, groups, lambda r: c2(r).wait_send())
    loop(1, group, lambda r: c3(r).wait_send())
    loop(0, blocks, lambda j: o_copy(j).wait())


def solution(mesh, group=GROUP, interpret=False):
    n = mesh.shape["seq"]

    def local(inner, gate, proj, raw, conv_weight, conv_bias, step_bias, rate, skip, gain):
        rows, width = inner.shape
        heads = width // HEAD
        blocks = width // LANES
        per = blocks // group
        groups = n // group
        states = proj.shape[1] // 4
        taps = conv_weight.shape[1]
        dma = pltpu.SemaphoreType.DMA
        vm = pltpu.VMEM
        scratch = [
            vm((blocks, rows, LANES), BF16),
            vm((blocks, rows, LANES), BF16),
            vm((blocks, rows, LANES), BF16),
            vm((blocks, rows + 16, LANES), F32),
            vm((blocks, rows, LANES), BF16),
            vm((blocks, rows, LANES), BF16),
            vm((blocks, rows, LANES), BF16),
            vm((blocks, rows, LANES), BF16),
            vm((blocks, rows, LANES), F32),
            vm((blocks, rows, LANES), F32),
            vm((blocks, rows, LANES), F32),
            vm(proj.shape, BF16),
            vm(raw.shape, BF16),
            vm(conv_weight.shape, F32),
            vm(conv_bias.shape, F32),
            vm(step_bias.shape, F32),
            vm(rate.shape, F32),
            vm(skip.shape, F32),
            vm((1, width), F32),
            vm((2 * rows, 2 * heads), BF16),
            vm((2 * rows + 16, 2 * heads), BF16),
            vm((48, 2 * heads), BF16),
            vm((rows, rows), BF16),
            vm((rows, rows), BF16),
            vm((2, states, rows), BF16),
            vm((2, rows, states), BF16),
            vm((8, width), BF16),
            vm((8, width), BF16),
            vm((8, LANES), F32),
            vm((group, 8, LANES), F32),
            vm((8, LANES), F32),
            vm((groups, 8, LANES), F32),
            vm((group, per, 2 * states, LANES), BF16),
            vm((group, per, 2 * states, LANES), BF16),
            vm((2, per, states, LANES), BF16),
            vm((groups, per, states, LANES), BF16),
            vm((group, per, 2 * states, LANES), BF16),
            vm((group, per, 2 * states, LANES), BF16),
            vm((rows, LANES), F32),
            dma((blocks,)),
            dma((blocks,)),
            dma((blocks,)),
            dma((8,)),
            dma((2,)),
            dma((2,)),
        ]
        near, far = dma((group - 1,)), dma((groups - 1,))
        scratch += [near, near, far, far, near, near, far, far, near, near]
        return pl.pallas_call(
            functools.partial(kernel, n, group, heads, taps),
            out_shape=jax.ShapeDtypeStruct((rows, width), BF16),
            in_specs=[pl.BlockSpec(memory_space=pl.ANY)] * 10,
            out_specs=pl.BlockSpec(memory_space=pl.ANY),
            scratch_shapes=scratch,
            compiler_params=pltpu.CompilerParams(
                collective_id=0, has_side_effects=True, vmem_limit_bytes=56 * 2**20
            ),
            name="mixer",
            interpret=interpret,
        )(
            inner, gate, proj, raw, conv_weight, conv_bias, step_bias, rate, skip,
            gain.reshape(1, width),
        )

    spec = P(("img", "seq"), None)
    return jax.shard_map(
        local,
        mesh=mesh,
        in_specs=(spec, spec, spec, spec, P(), P(), P(), P(), P(), P()),
        out_specs=spec,
        check_vma=False,
    )
```

time: 278 us -> 50.1 us (0.18)
  blocking collectives: 116 us -> 0 us
  waiting for transfers between devices: 54.2 us -> 0 us
  local copies, waits for them, and re-layouts: 51.5 us -> 4.22 us
  Pallas kernels: 0 us -> 45.4 us
  matrix products: 20.5 us -> 0 us
  other arithmetic: 15 us -> 0 us
  between operations: 14.1 us -> 0.01 us
  starting transfers between devices: 4.41 us -> 0 us
    all_gather x6 -> x0, blocking collectives: 116 us -> none  [carried_in(): pieces = jax.tree.map(lambda part: lax.all_gather(part, axis), running)]
    all_gather x2 -> x0, waiting for transfers between devices: 54.2 us -> none  [carried_in(): pieces = jax.tree.map(lambda part: lax.all_gather(part, axis), running)]
    pallas_call x0 -> x1, Pallas kernels: none -> 45.4 us  [local(): pl.pallas_call(functools.partial(kernel, n, group, heads, taps), out_shap...]
    slice x12 -> x0, local copies, waits for them, and re-layouts: 39.6 us -> none  [the longest x5 36.5 us: convolve(): window[start:start + length].astype(jnp.float32)]
    dot_general x8 -> x0, matrix products: 20.5 us -> none  [the longest x2 13 us: inter_terms(): jnp.einsum('tn,hpn->thp', read_rows.astype(jnp.float32), incoming, precis...]
    convert_element_type x4 -> x0, other arithmetic: 6.23 us -> none  [the longest x2 5.12 us: convolve(): return jax.nn.silu(accum).astype(jnp.bfloat16)]
    ppermute x2 -> x0, starting transfers between devices: 4.33 us -> none  [the longest x1 3.05 us: extended(): lax.ppermute(tail, axis, [(i, (i + 1) % count) for i in range(ends)])]
    reshape x2 -> x0, local copies, waits for them, and re-layouts: 3.75 us -> none  [the longest x1 1.87 us: local(): backward = (backward_base + inter_terms(backward_log, flipped_proj[:, 3 *...]
  transfers between devices with their start and end apart: 4 -> 0, of which waited for: 1 -> 0; matrix products, arithmetic and copies ran while one was open for 14% -> 0% of each run, Pallas kernels for 0% -> 0%
where the time goes in v1:
time: 50.1 us; the launch traced here: 49.7 us
  Pallas kernels  45.4 us (91%)
  local copies, waits for them, and re-layouts  4.22 us (8%)
    pallas_call x1, Pallas kernels, local(): pl.pallas_call(functools.partial(kernel, n, group, heads, taps), out_shap...  45.4 us
    unnamed x5, local copies, waits for them, and re-layouts  4.22 us

profile of v1, /device:TPU:24, one launch (start us, length us, event | category | flops | bytes accessed | tf_op | source)
XLA Modules:
  0.0 49.7 jit_solution(16102485903737918897)
XLA Ops:
  0.0 0.0 copy-start
  0.0 1.4 %copy.11.proj_hbm = bf16[128,64]{1,0:T(8,128)(2,1)} copy(bf16[128,64]{0,1:T(8,128)(2,1)} %param.12) | data formatting | bytes 32768 | tf_op args[2]
  1.4 0.0 copy-done
  1.4 0.7 %copy.12.raw_hbm = bf16[128,96]{1,0:T(8,128)(2,1)} copy(bf16[128,96]{0,1:T(8,128)(2,1)S(1)} %copy-done) | data formatting | bytes 49152 | tf_op args[3]
  2.2 45.4 %mixer.1 = bf16[128,3072]{1,0:T(8,128)(2,1)} custom-call(bf16[128,3072]{1,0:T(8,128)(2,1)} %x_hbm.1, bf16[128,3072]{1,0:T(8,128)(2,1)} %gate_hbm.1, bf16[128,64]{1,0:T(8,128)(2,1)} %copy.11.proj_hbm, bf16[128,96]{1,0:T(8,128)(2,1)} %copy.12.raw_hbm, f32[2,4,3072]{2,1,0:T(4,128)} %cw_hbm.1, f32[2,3072]{1,0:T(2,128)} %cb_hbm.1, f32[2,48]{1,0:T(2,128)} %sb_hbm.1, ...), custom_call_target="tpu_custom_call" | custom-call | tf_op jit(solution)/shard_map/mixer/pallas_call | solution.py:446
  47.6 2.1 %copy.14 = bf16[128,3072]{1,0:T(8,128)(2,1)} copy(bf16[128,3072]{1,0:T(8,128)(2,1)} %mixer.1) | data formatting | bytes 1572864
Async XLA Ops:
  0.0 1.4 %copy-start = (bf16[128,96]{0,1:T(8,128)(2,1)S(1)}, bf16[128,96]{0,1:T(8,128)(2,1)}, u32[]{:S(2)}) copy-start(bf16[128,96]{0,1:T(8,128)(2,1)} %param.13) | copy-start | bytes 73732

commit v2 on v1

--- a/solution.py
+++ b/solution.py
@@ -39,21 +39,21 @@
 
 def kernel(
     n, group, heads, kernel_taps,
-    x_hbm, gate_hbm, proj_hbm, raw_hbm, cw_hbm, cb_hbm, sb_hbm, rate_hbm, skip_hbm, gain_hbm,
-    out_hbm,
-    xb, gb, ob, xs, cf, cr, gf, gr, u, ef, er,
-    proj_v, raw_v, cw_v, cb_v, sb_v, rate_v, skip_v, gain_v,
-    lhs_g, lhs_e, lhs_x, mf, mr, bt, cm,
+    x_hbm, gate_hbm, proj_hbm, raw_hbm, cw_hbm, cb_hbm, sb_hbm, rate_hbm, skip_hbm,
+    u, sumsq,
+    xb, gb, xs, cf, cr, gf, gr, sg, ef, er, end0, gx, ext,
+    proj_v, raw_v, cw_v, cb_v, sb_v, rate_v, skip_v,
+    lhs_g, lhs_e, mf, mr, btm, bte, cm,
     prev_v, next_v, tot_v, tots_v, totg_v, totr_v,
-    send1, recv1, send2, recv2, send3, recv3, sumsq,
-    x_sem, g_sem, o_sem, s_sem, h_send, h_recv,
+    send1, recv1, send2, recv2, send3, recv3,
+    x_sem, g_sem, s_sem, h_send, h_recv,
     t1_send, t1_recv, t2_send, t2_recv, c1_send, c1_recv, c2_send, c2_recv, c3_send, c3_recv,
 ):
     rows = xb.shape[1]
     blocks = xb.shape[0]
     per = blocks // group
     groups = n // group
-    states = bt.shape[1]
+    states = btm.shape[1]
     me = lax.axis_index("seq")
     mem = lax.rem(me, group)
     grp = lax.div(me, group)
@@ -70,7 +70,7 @@
 
     small = [
         (raw_hbm, raw_v), (sb_hbm, sb_v), (rate_hbm, rate_v), (proj_hbm, proj_v),
-        (skip_hbm, skip_v), (cw_hbm, cw_v), (cb_hbm, cb_v), (gain_hbm, gain_v),
+        (skip_hbm, skip_v), (cw_hbm, cw_v), (cb_hbm, cb_v),
     ]
     loads = [pltpu.make_async_copy(a, b, s_sem.at[i]) for i, (a, b) in enumerate(small)]
     for copy in loads:
@@ -81,9 +81,6 @@
 
     def g_copy(j):
         return pltpu.make_async_copy(gate_hbm.at[:, lanes(j)], gb.at[j], g_sem.at[j])
-
-    def o_copy(j):
-        return pltpu.make_async_copy(ob.at[j], out_hbm.at[:, lanes(j)], o_sem.at[j])
 
     def start_x(j, carry):
         x_copy(j).start()
@@ -120,39 +117,45 @@
     for copy in loads:
         copy.wait()
 
-    later = lax.broadcasted_iota(jnp.int32, (rows, rows), 0)
-    earlier = lax.broadcasted_iota(jnp.int32, (rows, rows), 1)
-    masks = (later >= earlier, later <= earlier)
+    first_t = lax.broadcasted_iota(jnp.int32, (rows, rows), 0)
+    second_t = lax.broadcasted_iota(jnp.int32, (rows, rows), 1)
+    masks = (first_t >= second_t, first_t <= second_t)
     lasts = (rows - 1, 0)
+    column = lax.broadcasted_iota(jnp.int32, (states, rows), 1)
+    edge_rows = (column < 16, column >= rows - 16)
     raw = raw_v[...].astype(F32)
-    proj = proj_v[...].astype(F32)
-    proj_t = proj.T
-    zeros = jnp.zeros((16 - 2, heads), F32)
+    params = jnp.concatenate(
+        [
+            jnp.concatenate([sb_v[...], rate_v[...], jnp.zeros((4, heads), F32)], axis=0),
+            jnp.zeros((8, LANES - heads), F32),
+        ],
+        axis=1,
+    ).T
+    zeros = jnp.zeros((16 - 4, heads), F32)
     grow, decay, total, skips = [], [], [], []
     for d in range(2):
-        v = raw[:, d * heads : (d + 1) * heads] + sb_v[d : d + 1, :]
+        v = raw[d * heads : (d + 1) * heads] + params[:heads, d : d + 1]
         step = jnp.maximum(v, 0.0) + jnp.log1p(jnp.exp(-jnp.abs(v)))
-        tri = jnp.where(masks[d], 1.0, 0.0)
         cumul = jnp.dot(
-            tri, -rate_v[d : d + 1, :] * step, precision=lax.Precision.HIGHEST,
+            -params[:heads, 2 + d : 3 + d] * step,
+            jnp.where(masks[1 - d], 1.0, 0.0),
+            precision=lax.Precision.HIGHEST,
             preferred_element_type=F32,
         )
-        grow.append(jnp.exp(-cumul) * step)
-        decay.append(jnp.exp(cumul))
-        total.append(jnp.exp(cumul[lasts[d] : lasts[d] + 1, :]))
+        grow.append((jnp.exp(-cumul) * step).T)
+        decay.append(jnp.exp(cumul).T)
+        total.append(decay[d][lasts[d] : lasts[d] + 1, :])
         skips.append(skip_v[d : d + 1, :])
         first = 2 * d * states
-        write_t = proj_t[first : first + states, :].astype(BF16)
-        read = proj[:, first + states : first + 2 * states].astype(BF16)
-        bt[d] = write_t
+        write_t = proj_v[first : first + states, :]
+        read = proj_v[first + states : first + 2 * states, :].astype(F32).T.astype(BF16)
+        btm[d] = jnp.where(edge_rows[d], 0.0, write_t.astype(F32)).astype(BF16)
+        bte[d] = (write_t[:, :16], write_t[:, rows - 16 :])[d]
         cm[d] = read
         scores = jnp.where(masks[d], dot(read, write_t), 0.0).astype(BF16)
         (mf, mr)[d][...] = scores
-    lhs_g[...] = split(jnp.concatenate(grow, axis=0))
-    lhs_e[...] = split(jnp.concatenate(decay + skips + [zeros], axis=0))
-    lhs_x[...] = split(
-        jnp.concatenate([grow[0][:16], grow[1][rows - 16 :]] + total + [zeros], axis=0)
-    )
+    lhs_g[...] = split(jnp.concatenate(grow + total + skips + [zeros], axis=0))
+    lhs_e[...] = split(jnp.concatenate(decay, axis=0))
     tot_v[...] = jnp.concatenate(
         [
             jnp.concatenate(total + [jnp.zeros((6, heads), F32)], axis=0),
@@ -174,11 +177,15 @@
         xs[j, pl.ds(8 + rows, 8), :] = jnp.zeros((8, LANES), F32)
         xs[j, pl.ds(8, rows), :] = xb[j].astype(F32)
         wide = dot(lhs_g[...], spreader(j, heads, 2 * heads))
+        gx[j, pl.ds(0, 16), :] = wide[:16]
+        gx[j, pl.ds(16, 16), :] = wide[2 * rows - 16 : 2 * rows]
+        ext[j] = wide[2 * rows : 2 * rows + 8]
         for d in range(2):
             conved = taps(d, j, 0, rows)
             (cf, cr)[d][j] = conved
-            scaled = wide[d * rows : (d + 1) * rows] * conved.astype(F32)
-            (gf, gr)[d][j] = scaled.astype(BF16)
+            scaled = (wide[d * rows : (d + 1) * rows] * conved.astype(F32)).astype(BF16)
+            (gf, gr)[d][j] = scaled
+            end0[j, pl.ds(d * states, states), :] = dot(btm[d], scaled)
         return carry
 
     lax.fori_loop(0, blocks, conv, 0)
@@ -187,12 +194,12 @@
     edge = 8
     halo = [
         pltpu.make_async_remote_copy(
-            src_ref=x_hbm.at[pl.ds(rows - edge, edge)], dst_ref=prev_v,
+            src_ref=xb.at[:, pl.ds(rows - edge, edge), :], dst_ref=prev_v,
             send_sem=h_send.at[0], recv_sem=h_recv.at[0],
             device_id={"seq": after}, device_id_type=MESH,
         ),
         pltpu.make_async_remote_copy(
-            src_ref=x_hbm.at[pl.ds(0, edge)], dst_ref=next_v,
+            src_ref=xb.at[:, pl.ds(0, edge), :], dst_ref=next_v,
             send_sem=h_send.at[1], recv_sem=h_recv.at[1],
             device_id={"seq": before}, device_id_type=MESH,
         ),
@@ -238,42 +245,18 @@
     loop(1, group, lambda r: t1(r).start())
     tots_v[mem] = tot_v[...]
 
-    for copy in halo:
-        copy.wait()
+    def outside(j, carry):
+        g_copy(j).wait()
+        wide = dot(lhs_e[...], spreader(j, heads, 2 * heads))
+        gate = silu(gb[j].astype(F32))
+        sg[j] = gate
+        ef[j] = wide[:rows] * gate
+        er[j] = wide[rows:] * gate
+        return carry
+
+    lax.fori_loop(0, blocks, outside, 0)
+
     loop(1, group, lambda r: t1(r).wait())
-
-    def edges(j, carry):
-        has_before = jnp.where(me > 0, 1.0, 0.0)
-        has_after = jnp.where(me < n - 1, 1.0, 0.0)
-        xs[j, pl.ds(0, 8), :] = prev_v[:, lanes(j)].astype(F32) * has_before
-        xs[j, pl.ds(8 + rows, 8), :] = next_v[:, lanes(j)].astype(F32) * has_after
-        return carry
-
-    lax.fori_loop(0, blocks, edges, 0)
-
-    def finish(j, place, buffer):
-        wide = dot(lhs_x[...], spreader(j, heads, 2 * heads))
-        ends = []
-        for d in range(2):
-            first = (0, rows - 16)[d]
-            conved = taps(d, j, first, 16)
-            (cf, cr)[d][j, pl.ds(first, 16), :] = conved
-            scaled = wide[d * 16 : (d + 1) * 16] * conved.astype(F32)
-            (gf, gr)[d][j, pl.ds(first, 16), :] = scaled.astype(BF16)
-            end = dot(bt[d], (gf, gr)[d][j]) * wide[32 + d : 33 + d]
-            ends.append(end)
-        buffer[place] = jnp.concatenate(ends, axis=0).astype(BF16)
-
-    def ends(r):
-        owner = member(r)
-        for b in range(per):
-            finish(owner * per + b, (owner, b), send1)
-        c1(r).start()
-
-    loop(1, group, ends)
-    for b in range(per):
-        finish(mem * per + b, (mem, b), recv1)
-
     product = tots_v[0]
     for m in range(1, group):
         product = product * tots_v[m]
@@ -281,19 +264,48 @@
     loop(1, groups, lambda r: t2(r).start())
     totr_v[grp] = product
 
+    for copy in halo:
+        copy.wait()
+
+    def edges(j, carry):
+        has_before = jnp.where(me > 0, 1.0, 0.0)
+        has_after = jnp.where(me < n - 1, 1.0, 0.0)
+        xs[j, pl.ds(0, 8), :] = prev_v[j].astype(F32) * has_before
+        xs[j, pl.ds(8 + rows, 8), :] = next_v[j].astype(F32) * has_after
+        return carry
+
+    lax.fori_loop(0, blocks, edges, 0)
+
+    def finish(owner, buffer):
+        results = []
+        for b in range(per):
+            j = owner * per + b
+            for d in range(2):
+                first = (0, rows - 16)[d]
+                conved = taps(d, j, first, 16)
+                scaled = (gx[j, pl.ds(16 * d, 16), :] * conved.astype(F32)).astype(BF16)
+                end = end0[j, pl.ds(d * states, states), :] + dot(bte[d], scaled)
+                end = (end * ext[j, pl.ds(d, 1), :]).astype(BF16)
+                results.append((b, j, d, first, conved, scaled, end))
+        for b, j, d, first, conved, scaled, end in results:
+            (cf, cr)[d][j, pl.ds(first, 16), :] = conved
+            (gf, gr)[d][j, pl.ds(first, 16), :] = scaled
+            buffer[owner, b, pl.ds(d * states, states), :] = end
+
+    def ends(r):
+        owner = member(r)
+        finish(owner, send1)
+        c1(r).start()
+
+    loop(1, group, ends)
+    finish(mem, recv1)
+
     def inner(j, carry):
-        g_copy(j).wait()
-        wide = dot(lhs_e[...], spreader(j, heads, 2 * heads))
-        gate = silu(gb[j].astype(F32))
-        far_f, far_r = wide[:rows] * gate, wide[rows : 2 * rows] * gate
-        ef[j] = far_f
-        er[j] = far_r
         direct = (
-            wide[2 * rows : 2 * rows + 1] * cf[j].astype(F32)
-            + wide[2 * rows + 1 : 2 * rows + 2] * cr[j].astype(F32)
+            ext[j, pl.ds(2, 1), :] * cf[j].astype(F32) + ext[j, pl.ds(3, 1), :] * cr[j].astype(F32)
         )
         u[j] = (
-            direct * gate + far_f * dot(mf[...], gf[j]) + far_r * dot(mr[...], gr[j])
+            direct * sg[j] + ef[j] * dot(mf[...], gf[j]) + er[j] * dot(mr[...], gr[j])
         )
         return carry
 
@@ -366,22 +378,30 @@
         outer(lax.rem(mem + group - r, group))
 
     loop(1, group, arrived)
-    mean = jnp.sum(sumsq[...], axis=1, keepdims=True) * (1.0 / (blocks * LANES))
-    scale = lax.rsqrt(mean + 1e-05)
-
-    def write(j, carry):
-        ob[j] = (u[j] * scale * gain_v[:, lanes(j)]).astype(BF16)
-        o_copy(j).start()
-        return carry
-
-    lax.fori_loop(0, blocks, write, 0)
     loop(1, group, lambda r: c1(r).wait_send())
     loop(1, groups, lambda r: c2(r).wait_send())
     loop(1, group, lambda r: c3(r).wait_send())
-    loop(0, blocks, lambda j: o_copy(j).wait())
-
-
-def solution(mesh, group=GROUP, interpret=False):
+
+
+def finale(u, sumsq, gain_hbm, out_hbm, ob, gain_v, o_sem, s_sem):
+    blocks = ob.shape[0]
+    load = pltpu.make_async_copy(gain_hbm, gain_v, s_sem)
+    load.start()
+    mean = jnp.sum(sumsq[...], axis=1, keepdims=True) * (1.0 / (blocks * LANES))
+    scale = lax.rsqrt(mean + 1e-05)
+    load.wait()
+
+    def o_copy(j):
+        return pltpu.make_async_copy(ob.at[j], out_hbm.at[:, pl.ds(j * LANES, LANES)], o_sem.at[j])
+
+    for j in range(blocks):
+        ob[j] = (u[j] * scale * gain_v[:, pl.ds(j * LANES, LANES)]).astype(BF16)
+        o_copy(j).start()
+    for j in range(blocks):
+        o_copy(j).wait()
+
+
+def solution(mesh, group=GROUP):
     n = mesh.shape["seq"]
 
     def local(inner, gate, proj, raw, conv_weight, conv_bias, step_bias, rate, skip, gain):
@@ -394,35 +414,38 @@
         taps = conv_weight.shape[1]
         dma = pltpu.SemaphoreType.DMA
         vm = pltpu.VMEM
+        wide16 = vm((blocks, rows, LANES), BF16)
+        wide32 = vm((blocks, rows, LANES), F32)
         scratch = [
-            vm((blocks, rows, LANES), BF16),
-            vm((blocks, rows, LANES), BF16),
-            vm((blocks, rows, LANES), BF16),
+            wide16,
+            wide16,
             vm((blocks, rows + 16, LANES), F32),
-            vm((blocks, rows, LANES), BF16),
-            vm((blocks, rows, LANES), BF16),
-            vm((blocks, rows, LANES), BF16),
-            vm((blocks, rows, LANES), BF16),
-            vm((blocks, rows, LANES), F32),
-            vm((blocks, rows, LANES), F32),
-            vm((blocks, rows, LANES), F32),
-            vm(proj.shape, BF16),
-            vm(raw.shape, BF16),
+            wide16,
+            wide16,
+            wide16,
+            wide16,
+            wide32,
+            wide32,
+            wide32,
+            vm((blocks, 2 * states, LANES), F32),
+            vm((blocks, 32, LANES), F32),
+            vm((blocks, 8, LANES), F32),
+            vm(proj.shape[::-1], BF16),
+            vm(raw.shape[::-1], BF16),
             vm(conv_weight.shape, F32),
             vm(conv_bias.shape, F32),
             vm(step_bias.shape, F32),
             vm(rate.shape, F32),
             vm(skip.shape, F32),
-            vm((1, width), F32),
+            vm((2 * rows + 16, 2 * heads), BF16),
             vm((2 * rows, 2 * heads), BF16),
-            vm((2 * rows + 16, 2 * heads), BF16),
-            vm((48, 2 * heads), BF16),
             vm((rows, rows), BF16),
             vm((rows, rows), BF16),
             vm((2, states, rows), BF16),
+            vm((2, states, 16), BF16),
             vm((2, rows, states), BF16),
-            vm((8, width), BF16),
-            vm((8, width), BF16),
+            vm((blocks, 8, LANES), BF16),
+            vm((blocks, 8, LANES), BF16),
             vm((8, LANES), F32),
             vm((group, 8, LANES), F32),
             vm((8, LANES), F32),
@@ -433,8 +456,6 @@
             vm((groups, per, states, LANES), BF16),
             vm((group, per, 2 * states, LANES), BF16),
             vm((group, per, 2 * states, LANES), BF16),
-            vm((rows, LANES), F32),
-            dma((blocks,)),
             dma((blocks,)),
             dma((blocks,)),
             dma((8,)),
@@ -443,21 +464,38 @@
         ]
         near, far = dma((group - 1,)), dma((groups - 1,))
         scratch += [near, near, far, far, near, near, far, far, near, near]
-        return pl.pallas_call(
+        vmem = pl.BlockSpec(memory_space=pltpu.VMEM)
+        hbm = pl.BlockSpec(memory_space=pl.ANY)
+        gated, sumsq = pl.pallas_call(
             functools.partial(kernel, n, group, heads, taps),
-            out_shape=jax.ShapeDtypeStruct((rows, width), BF16),
-            in_specs=[pl.BlockSpec(memory_space=pl.ANY)] * 10,
-            out_specs=pl.BlockSpec(memory_space=pl.ANY),
+            out_shape=(
+                jax.ShapeDtypeStruct((blocks, rows, LANES), F32),
+                jax.ShapeDtypeStruct((rows, LANES), F32),
+            ),
+            in_specs=[hbm] * 9,
+            out_specs=(vmem, vmem),
             scratch_shapes=scratch,
             compiler_params=pltpu.CompilerParams(
-                collective_id=0, has_side_effects=True, vmem_limit_bytes=56 * 2**20
+                collective_id=0, has_side_effects=True, vmem_limit_bytes=36 * 2**20
             ),
             name="mixer",
-            interpret=interpret,
         )(
-            inner, gate, proj, raw, conv_weight, conv_bias, step_bias, rate, skip,
-            gain.reshape(1, width),
-        )
+            *(
+                pltpu.with_memory_space_constraint(array, pltpu.HBM)
+                for array in (
+                    inner, gate, proj.T, raw.T, conv_weight, conv_bias, step_bias, rate, skip
+                )
+            )
+        )
+        return pl.pallas_call(
+            finale,
+            out_shape=jax.ShapeDtypeStruct((rows, width), BF16),
+            in_specs=[vmem, vmem, hbm],
+            out_specs=hbm,
+            scratch_shapes=[wide16, vm((1, width), F32), dma((blocks,)), dma],
+            compiler_params=pltpu.CompilerParams(vmem_limit_bytes=16 * 2**20),
+            name="finale",
+        )(gated, sumsq, gain.reshape(1, width))
 
     spec = P(("img", "seq"), None)
     return jax.shard_map(

time: 50.1 us -> 46.1 us (0.920)
  local copies, waits for them, and re-layouts: 4.22 us -> 0.01 us
    unnamed x5 -> x2, local copies, waits for them, and re-layouts: 4.22 us -> 0.01 us
    pallas_call x0 -> x1, Pallas kernels: none -> 1.2 us  [local(): pl.pallas_call(finale, out_shape=jax.ShapeDtypeStruct((rows, width), BF16...]
    pallas_call x1, Pallas kernels: 45.4 us -> 44.5 us  [local(): pl.pallas_call(functools.partial(kernel, n, group, heads, taps), out_shap...]
where the time goes in v2:
time: 46.1 us; the launch traced here: 45.7 us
  Pallas kernels  45.7 us (99%)
    pallas_call x1, Pallas kernels, local(): pl.pallas_call(functools.partial(kernel, n, group, heads, taps), out_shap...  44.5 us
    pallas_call x1, Pallas kernels, local(): pl.pallas_call(finale, out_shape=jax.ShapeDtypeStruct((rows, width), BF16...  1.2 us

profile of v2, /device:TPU:24, one launch (start us, length us, event | category | flops | bytes accessed | tf_op | source)
XLA Modules:
  0.0 45.7 jit_solution(17107328106260319642)
XLA Ops:
  0.0 0.0 copy-start
  0.0 44.5 %mixer.1 = (f32[24,128,128]{2,1,0:T(8,128)S(1)}, f32[128,128]{1,0:T(8,128)S(1)}) custom-call(bf16[128,3072]{1,0:T(8,128)(2,1)} %x_hbm.1, bf16[128,3072]{1,0:T(8,128)(2,1)} %gate_hbm.1, bf16[64,128]{1,0:T(8,128)(2,1)} %bitcast.5, bf16[96,128]{1,0:T(8,128)(2,1)} %bitcast.4, f32[2,4,3072]{2,1,0:T(4,128)} %cw_hbm.1, f32[2,3072]{1,0:T(2,128)} %cb_hbm.1, ...), custom_call_target="tpu_custom_call" | custom-call | tf_op jit(solution)/shard_map/mixer/pallas_call | solution.py:469
  44.5 0.0 copy-done
  44.5 1.2 %finale.1 = bf16[128,3072]{1,0:T(8,128)(2,1)} custom-call(f32[24,128,128]{2,1,0:T(8,128)S(1)} %get-tuple-element.7.u, f32[128,128]{1,0:T(8,128)S(1)} %get-tuple-element.8.sumsq, f32[1,3072]{1,0:T(1,128)S(1)} %bitcast.3), custom_call_target="tpu_custom_call" | custom-call | tf_op jit(solution)/shard_map/finale/pallas_call | solution.py:490
Async XLA Ops:
  0.0 44.5 %copy-start = (f32[3072]{0:T(1024)S(1)}, f32[3072]{0:T(1024)}, u32[]{:S(2)}) copy-start(f32[3072]{0:T(1024)} %param.19) | copy-start | bytes 36868

commit v3 on v2

--- a/solution.py
+++ b/solution.py
@@ -13,6 +13,7 @@
 LANES = 128
 HEAD = 64
 GROUP = 8
+BAND = 32
 
 
 def split(v):
@@ -41,19 +42,19 @@
     n, group, heads, kernel_taps,
     x_hbm, gate_hbm, proj_hbm, raw_hbm, cw_hbm, cb_hbm, sb_hbm, rate_hbm, skip_hbm,
     u, sumsq,
-    xb, gb, xs, cf, cr, gf, gr, sg, ef, er, end0, gx, ext,
+    xb, gb, xs, cf, cr, gf, gr, sg, ef, er, gw, ext,
     proj_v, raw_v, cw_v, cb_v, sb_v, rate_v, skip_v,
-    lhs_g, lhs_e, mf, mr, btm, bte, cm,
+    lhs, mf, mr, bt, cm,
     prev_v, next_v, tot_v, tots_v, totg_v, totr_v,
     send1, recv1, send2, recv2, send3, recv3,
-    x_sem, g_sem, s_sem, h_send, h_recv,
+    x_sem, g_sem, s_sem, ready, h_send, h_recv,
     t1_send, t1_recv, t2_send, t2_recv, c1_send, c1_recv, c2_send, c2_recv, c3_send, c3_recv,
 ):
-    rows = xb.shape[1]
-    blocks = xb.shape[0]
+    rows = u.shape[1]
+    blocks = u.shape[0]
     per = blocks // group
     groups = n // group
-    states = btm.shape[1]
+    states = bt.shape[1]
     me = lax.axis_index("seq")
     mem = lax.rem(me, group)
     grp = lax.div(me, group)
@@ -67,6 +68,14 @@
 
     def far(r):
         return lax.rem(grp + r, groups)
+
+    def sweep(body, many):
+        def turn(i, carry):
+            for q in range(many):
+                body(i * many + q)
+            return carry
+
+        lax.fori_loop(0, blocks // many, turn, 0)
 
     small = [
         (raw_hbm, raw_v), (sb_hbm, sb_v), (rate_hbm, rate_v), (proj_hbm, proj_v),
@@ -76,44 +85,34 @@
     for copy in loads:
         copy.start()
 
-    def x_copy(j):
-        return pltpu.make_async_copy(x_hbm.at[:, lanes(j)], xb.at[j], x_sem.at[j])
-
-    def g_copy(j):
-        return pltpu.make_async_copy(gate_hbm.at[:, lanes(j)], gb.at[j], g_sem.at[j])
-
-    def start_x(j, carry):
-        x_copy(j).start()
-        return carry
-
-    lax.fori_loop(0, blocks, start_x, 0)
+    bands = rows // BAND
+
+    def x_copy(i):
+        band = pl.ds(i * BAND, BAND)
+        return pltpu.make_async_copy(x_hbm.at[band], xb.at[band], x_sem.at[i])
+
+    def g_copy(i):
+        band = pl.ds(i * BAND, BAND)
+        return pltpu.make_async_copy(gate_hbm.at[band], gb.at[band], g_sem.at[i])
+
+    for i in range(bands):
+        x_copy(i).start()
 
     barrier = pltpu.get_barrier_semaphore()
     after = lax.rem(me + 1, n)
     before = lax.rem(me + n - 1, n)
-    for peer in (after, before):
-        pl.semaphore_signal(barrier, inc=1, device_id={"seq": peer}, device_id_type=MESH)
-
-    def greet_group(r, carry):
-        pl.semaphore_signal(
-            barrier, inc=1, device_id={"seq": base + member(r)}, device_id_type=MESH
-        )
-        return carry
-
-    def greet_far(r, carry):
-        pl.semaphore_signal(
-            barrier, inc=1, device_id={"seq": far(r) * group + mem}, device_id_type=MESH
-        )
-        return carry
-
-    lax.fori_loop(1, groups, greet_far, 0)
-    lax.fori_loop(1, group, greet_group, 0)
-
-    def start_g(j, carry):
-        g_copy(j).start()
-        return carry
-
-    lax.fori_loop(0, blocks, start_g, 0)
+    beside = (lax.rem(me + group, n), lax.rem(me + n - group, n))
+
+    def signal(semaphore, peer):
+        pl.semaphore_signal(semaphore, inc=1, device_id={"seq": peer}, device_id_type=MESH)
+
+    for peer in (after, before) + beside:
+        signal(barrier, peer)
+    for r in range(1, group):
+        signal(barrier, base + member(r))
+
+    for i in range(bands):
+        g_copy(i).start()
     for copy in loads:
         copy.wait()
 
@@ -121,8 +120,6 @@
     second_t = lax.broadcasted_iota(jnp.int32, (rows, rows), 1)
     masks = (first_t >= second_t, first_t <= second_t)
     lasts = (rows - 1, 0)
-    column = lax.broadcasted_iota(jnp.int32, (states, rows), 1)
-    edge_rows = (column < 16, column >= rows - 16)
     raw = raw_v[...].astype(F32)
     params = jnp.concatenate(
         [
@@ -149,13 +146,11 @@
         first = 2 * d * states
         write_t = proj_v[first : first + states, :]
         read = proj_v[first + states : first + 2 * states, :].astype(F32).T.astype(BF16)
-        btm[d] = jnp.where(edge_rows[d], 0.0, write_t.astype(F32)).astype(BF16)
-        bte[d] = (write_t[:, :16], write_t[:, rows - 16 :])[d]
+        bt[d] = write_t
         cm[d] = read
         scores = jnp.where(masks[d], dot(read, write_t), 0.0).astype(BF16)
         (mf, mr)[d][...] = scores
-    lhs_g[...] = split(jnp.concatenate(grow + total + skips + [zeros], axis=0))
-    lhs_e[...] = split(jnp.concatenate(decay, axis=0))
+    lhs[...] = split(jnp.concatenate(decay + grow + total + skips + [zeros], axis=0))
     tot_v[...] = jnp.concatenate(
         [
             jnp.concatenate(total + [jnp.zeros((6, heads), F32)], axis=0),
@@ -164,42 +159,28 @@
         axis=1,
     )
 
-    def taps(d, j, first, count):
-        acc = jnp.zeros((count, LANES), F32) + cb_v[d : d + 1, lanes(j)]
-        for k in range(kernel_taps):
-            shift = -k if d == 0 else k
-            acc = acc + cw_v[d, k : k + 1, lanes(j)] * xs[j, pl.ds(8 + first + shift, count), :]
-        return silu(acc).astype(BF16)
-
-    def conv(j, carry):
-        x_copy(j).wait()
-        xs[j, pl.ds(0, 8), :] = jnp.zeros((8, LANES), F32)
-        xs[j, pl.ds(8 + rows, 8), :] = jnp.zeros((8, LANES), F32)
-        xs[j, pl.ds(8, rows), :] = xb[j].astype(F32)
-        wide = dot(lhs_g[...], spreader(j, heads, 2 * heads))
-        gx[j, pl.ds(0, 16), :] = wide[:16]
-        gx[j, pl.ds(16, 16), :] = wide[2 * rows - 16 : 2 * rows]
-        ext[j] = wide[2 * rows : 2 * rows + 8]
-        for d in range(2):
-            conved = taps(d, j, 0, rows)
-            (cf, cr)[d][j] = conved
-            scaled = (wide[d * rows : (d + 1) * rows] * conved.astype(F32)).astype(BF16)
-            (gf, gr)[d][j] = scaled
-            end0[j, pl.ds(d * states, states), :] = dot(btm[d], scaled)
-        return carry
-
-    lax.fori_loop(0, blocks, conv, 0)
-
-    pl.semaphore_wait(barrier, 2 + (groups - 1) + (group - 1))
+    for i in range(bands):
+        x_copy(i).wait()
+    pl.semaphore_wait(barrier, 4 + (group - 1))
+    rounds = groups // 2 - 1
+
+    def relay(k):
+        if 0 < k <= rounds:
+            pl.semaphore_wait(ready.at[k - 1], 2)
+        if k < rounds:
+            for peer in beside:
+                signal(ready.at[k], peer)
+
+    relay(0)
     edge = 8
     halo = [
         pltpu.make_async_remote_copy(
-            src_ref=xb.at[:, pl.ds(rows - edge, edge), :], dst_ref=prev_v,
+            src_ref=xb.at[pl.ds(rows - edge, edge)], dst_ref=prev_v,
             send_sem=h_send.at[0], recv_sem=h_recv.at[0],
             device_id={"seq": after}, device_id_type=MESH,
         ),
         pltpu.make_async_remote_copy(
-            src_ref=xb.at[:, pl.ds(0, edge), :], dst_ref=next_v,
+            src_ref=xb.at[pl.ds(0, edge)], dst_ref=next_v,
             send_sem=h_send.at[1], recv_sem=h_recv.at[1],
             device_id={"seq": before}, device_id_type=MESH,
         ),
@@ -245,71 +226,82 @@
     loop(1, group, lambda r: t1(r).start())
     tots_v[mem] = tot_v[...]
 
-    def outside(j, carry):
-        g_copy(j).wait()
-        wide = dot(lhs_e[...], spreader(j, heads, 2 * heads))
-        gate = silu(gb[j].astype(F32))
+    for i in range(bands):
+        g_copy(i).wait()
+
+    def outside(j):
+        wide = dot(lhs[...], spreader(j, heads, 2 * heads))
+        gate = silu(gb[:, lanes(j)].astype(F32))
         sg[j] = gate
         ef[j] = wide[:rows] * gate
-        er[j] = wide[rows:] * gate
-        return carry
-
-    lax.fori_loop(0, blocks, outside, 0)
+        er[j] = wide[rows : 2 * rows] * gate
+        gw[0, j] = wide[2 * rows : 3 * rows]
+        gw[1, j] = wide[3 * rows : 4 * rows]
+        ext[j] = wide[4 * rows : 4 * rows + 8]
+
+    sweep(outside, 3)
+    for copy in halo:
+        copy.wait()
+
+    has_before = jnp.where(me > 0, 1.0, 0.0)
+    has_after = jnp.where(me < n - 1, 1.0, 0.0)
+
+    def conv(owner):
+        for b in range(per):
+            j = owner * per + b
+            xs[j, pl.ds(0, 8), :] = prev_v[:, lanes(j)].astype(F32) * has_before
+            xs[j, pl.ds(8 + rows, 8), :] = next_v[:, lanes(j)].astype(F32) * has_after
+            xs[j, pl.ds(8, rows), :] = xb[:, lanes(j)].astype(F32)
+        for b in range(per):
+            j = owner * per + b
+            for d in range(2):
+                acc = 0.5 * cb_v[d : d + 1, lanes(j)]
+                for k in range(kernel_taps):
+                    shift = -k if d == 0 else k
+                    tap = 0.5 * cw_v[d, k : k + 1, lanes(j)]
+                    acc = acc + tap * xs[j, pl.ds(8 + shift, rows), :]
+                conved = (acc + acc * jnp.tanh(acc)).astype(BF16)
+                (cf, cr)[d][j] = conved
+                (gf, gr)[d][j] = (gw[d, j] * conved.astype(F32)).astype(BF16)
+
+    def finish(owner, buffer):
+        results = []
+        for b in range(per):
+            j = owner * per + b
+            for d in range(2):
+                end = dot(bt[d], (gf, gr)[d][j]) * ext[j, pl.ds(d, 1), :]
+                results.append((b, d, end.astype(BF16)))
+        for b, d, end in results:
+            buffer[owner, b, pl.ds(d * states, states), :] = end
+
+    conv(member(1))
+
+    def ends(r):
+        finish(member(r), send1)
+        conv(member(r + 1))
+        c1(r).start()
+
+    loop(1, group, ends)
+    finish(mem, recv1)
+    relay(1)
 
     loop(1, group, lambda r: t1(r).wait())
     product = tots_v[0]
     for m in range(1, group):
         product = product * tots_v[m]
     totg_v[...] = product
-    loop(1, groups, lambda r: t2(r).start())
     totr_v[grp] = product
 
-    for copy in halo:
-        copy.wait()
-
-    def edges(j, carry):
-        has_before = jnp.where(me > 0, 1.0, 0.0)
-        has_after = jnp.where(me < n - 1, 1.0, 0.0)
-        xs[j, pl.ds(0, 8), :] = prev_v[j].astype(F32) * has_before
-        xs[j, pl.ds(8 + rows, 8), :] = next_v[j].astype(F32) * has_after
-        return carry
-
-    lax.fori_loop(0, blocks, edges, 0)
-
-    def finish(owner, buffer):
-        results = []
-        for b in range(per):
-            j = owner * per + b
-            for d in range(2):
-                first = (0, rows - 16)[d]
-                conved = taps(d, j, first, 16)
-                scaled = (gx[j, pl.ds(16 * d, 16), :] * conved.astype(F32)).astype(BF16)
-                end = end0[j, pl.ds(d * states, states), :] + dot(bte[d], scaled)
-                end = (end * ext[j, pl.ds(d, 1), :]).astype(BF16)
-                results.append((b, j, d, first, conved, scaled, end))
-        for b, j, d, first, conved, scaled, end in results:
-            (cf, cr)[d][j, pl.ds(first, 16), :] = conved
-            (gf, gr)[d][j, pl.ds(first, 16), :] = scaled
-            buffer[owner, b, pl.ds(d * states, states), :] = end
-
-    def ends(r):
-        owner = member(r)
-        finish(owner, send1)
-        c1(r).start()
-
-    loop(1, group, ends)
-    finish(mem, recv1)
-
-    def inner(j, carry):
+    def inner(j):
         direct = (
             ext[j, pl.ds(2, 1), :] * cf[j].astype(F32) + ext[j, pl.ds(3, 1), :] * cr[j].astype(F32)
         )
         u[j] = (
             direct * sg[j] + ef[j] * dot(mf[...], gf[j]) + er[j] * dot(mr[...], gr[j])
         )
-        return carry
-
-    lax.fori_loop(0, blocks, inner, 0)
+
+    sweep(inner, 4)
+    relay(2)
 
     loop(1, group, lambda r: c1(r).wait_recv())
 
@@ -334,6 +326,8 @@
             run_r = run_r * near_t[b][8 * k + 1 : 8 * k + 2] + part(recv1, k, b, 1)
         send2[0, b] = run_f.astype(BF16)
         send2[1, b] = run_r.astype(BF16)
+    relay(3)
+    loop(1, groups, lambda r: t2(r).start())
     loop(1, groups, lambda r: c2(r).start())
     loop(1, groups, lambda r: t2(r).wait())
     far_t = [spread(totr_v, b) for b in range(per)]
@@ -384,21 +378,25 @@
 
 
 def finale(u, sumsq, gain_hbm, out_hbm, ob, gain_v, o_sem, s_sem):
-    blocks = ob.shape[0]
+    blocks, rows, _ = u.shape
     load = pltpu.make_async_copy(gain_hbm, gain_v, s_sem)
     load.start()
     mean = jnp.sum(sumsq[...], axis=1, keepdims=True) * (1.0 / (blocks * LANES))
     scale = lax.rsqrt(mean + 1e-05)
     load.wait()
 
-    def o_copy(j):
-        return pltpu.make_async_copy(ob.at[j], out_hbm.at[:, pl.ds(j * LANES, LANES)], o_sem.at[j])
-
-    for j in range(blocks):
-        ob[j] = (u[j] * scale * gain_v[:, pl.ds(j * LANES, LANES)]).astype(BF16)
-        o_copy(j).start()
-    for j in range(blocks):
-        o_copy(j).wait()
+    def o_copy(i):
+        band = pl.ds(i * BAND, BAND)
+        return pltpu.make_async_copy(ob.at[band], out_hbm.at[band], o_sem.at[i])
+
+    for i in range(rows // BAND):
+        part = slice(i * BAND, (i + 1) * BAND)
+        for j in range(blocks):
+            lanes = slice(j * LANES, (j + 1) * LANES)
+            ob[part, lanes] = (u[j, part] * scale[part] * gain_v[:, lanes]).astype(BF16)
+        o_copy(i).start()
+    for i in range(rows // BAND):
+        o_copy(i).wait()
 
 
 def solution(mesh, group=GROUP):
@@ -417,8 +415,8 @@
         wide16 = vm((blocks, rows, LANES), BF16)
         wide32 = vm((blocks, rows, LANES), F32)
         scratch = [
-            wide16,
-            wide16,
+            vm((rows, width), BF16),
+            vm((rows, width), BF16),
             vm((blocks, rows + 16, LANES), F32),
             wide16,
             wide16,
@@ -427,8 +425,7 @@
             wide32,
             wide32,
             wide32,
-            vm((blocks, 2 * states, LANES), F32),
-            vm((blocks, 32, LANES), F32),
+            vm((2, blocks, rows, LANES), F32),
             vm((blocks, 8, LANES), F32),
             vm(proj.shape[::-1], BF16),
             vm(raw.shape[::-1], BF16),
@@ -437,15 +434,13 @@
             vm(step_bias.shape, F32),
             vm(rate.shape, F32),
             vm(skip.shape, F32),
-            vm((2 * rows + 16, 2 * heads), BF16),
-            vm((2 * rows, 2 * heads), BF16),
+            vm((4 * rows + 16, 2 * heads), BF16),
             vm((rows, rows), BF16),
             vm((rows, rows), BF16),
             vm((2, states, rows), BF16),
-            vm((2, states, 16), BF16),
             vm((2, rows, states), BF16),
-            vm((blocks, 8, LANES), BF16),
-            vm((blocks, 8, LANES), BF16),
+            vm((8, width), BF16),
+            vm((8, width), BF16),
             vm((8, LANES), F32),
             vm((group, 8, LANES), F32),
             vm((8, LANES), F32),
@@ -456,9 +451,10 @@
             vm((groups, per, states, LANES), BF16),
             vm((group, per, 2 * states, LANES), BF16),
             vm((group, per, 2 * states, LANES), BF16),
-            dma((blocks,)),
-            dma((blocks,)),
+            dma((rows // BAND,)),
+            dma((rows // BAND,)),
             dma((8,)),
+            pltpu.SemaphoreType.REGULAR((max(1, groups // 2 - 1),)),
             dma((2,)),
             dma((2,)),
         ]
@@ -492,7 +488,9 @@
             out_shape=jax.ShapeDtypeStruct((rows, width), BF16),
             in_specs=[vmem, vmem, hbm],
             out_specs=hbm,
-            scratch_shapes=[wide16, vm((1, width), F32), dma((blocks,)), dma],
+            scratch_shapes=[
+                vm((rows, width), BF16), vm((1, width), F32), dma((rows // BAND,)), dma
+            ],
             compiler_params=pltpu.CompilerParams(vmem_limit_bytes=16 * 2**20),
             name="finale",
         )(gated, sumsq, gain.reshape(1, width))

time: 46.1 us -> 39.9 us (0.87)
  Pallas kernels: 45.7 us -> 39.7 us
    pallas_call x1, Pallas kernels: 44.5 us -> 38.7 us  [local(): pl.pallas_call(functools.partial(kernel, n, group, heads, taps), out_shap...]
where the time goes in v3:
time: 39.9 us; the launch traced here: 39.7 us
  Pallas kernels  39.7 us (99%)
    pallas_call x1, Pallas kernels, local(): pl.pallas_call(functools.partial(kernel, n, group, heads, taps), out_shap...  38.7 us
    pallas_call x1, Pallas kernels, local(): pl.pallas_call(finale, out_shape=jax.ShapeDtypeStruct((rows, width), BF16...  1.07 us

profile of v3, /device:TPU:24, one launch (start us, length us, event | category | flops | bytes accessed | tf_op | source)
XLA Modules:
  0.0 39.7 jit_solution(2322675905226444543)
XLA Ops:
  0.0 0.0 copy-start
  0.0 38.7 %mixer.1 = (f32[24,128,128]{2,1,0:T(8,128)S(1)}, f32[128,128]{1,0:T(8,128)S(1)}) custom-call(bf16[128,3072]{1,0:T(8,128)(2,1)} %x_hbm.1, bf16[128,3072]{1,0:T(8,128)(2,1)} %gate_hbm.1, bf16[64,128]{1,0:T(8,128)(2,1)} %bitcast.5, bf16[96,128]{1,0:T(8,128)(2,1)} %bitcast.4, f32[2,4,3072]{2,1,0:T(4,128)} %cw_hbm.1, f32[2,3072]{1,0:T(2,128)} %cb_hbm.1, ...), custom_call_target="tpu_custom_call" | custom-call | tf_op jit(solution)/shard_map/mixer/pallas_call | solution.py:465
  38.7 0.0 copy-done
  38.7 1.1 %finale.1 = bf16[128,3072]{1,0:T(8,128)(2,1)} custom-call(f32[24,128,128]{2,1,0:T(8,128)S(1)} %get-tuple-element.7.u, f32[128,128]{1,0:T(8,128)S(1)} %get-tuple-element.8.sumsq, f32[1,3072]{1,0:T(1,128)S(1)} %bitcast.3), custom_call_target="tpu_custom_call" | custom-call | tf_op jit(solution)/shard_map/finale/pallas_call | solution.py:486
Async XLA Ops:
  0.0 38.7 %copy-start = (f32[3072]{0:T(1024)S(1)}, f32[3072]{0:T(1024)}, u32[]{:S(2)}) copy-start(f32[3072]{0:T(1024)} %param.19) | copy-start | bytes 36868

commit v4 on v3

--- a/solution.py
+++ b/solution.py
@@ -13,6 +13,8 @@
 LANES = 128
 HEAD = 64
 GROUP = 8
+NEAR = (6, 5, 7, 2, 4, 1, 3)
+FAR = (4, 3, 5, 2, 6, 1, 7)
 BAND = 32
 
 
@@ -42,7 +44,7 @@
     n, group, heads, kernel_taps,
     x_hbm, gate_hbm, proj_hbm, raw_hbm, cw_hbm, cb_hbm, sb_hbm, rate_hbm, skip_hbm,
     u, sumsq,
-    xb, gb, xs, cf, cr, gf, gr, sg, ef, er, gw, ext,
+    xb, gb, xs, cf, cr, gf, gr, ef, er, gw, ext,
     proj_v, raw_v, cw_v, cb_v, sb_v, rate_v, skip_v,
     lhs, mf, mr, bt, cm,
     prev_v, next_v, tot_v, tots_v, totg_v, totr_v,
@@ -63,11 +65,24 @@
     def lanes(j):
         return pl.ds(pl.multiple_of(j * LANES, LANES), LANES)
 
+    def pick(table, r):
+        found = 0
+        for k, value in enumerate(table):
+            found = found + jnp.where(r == k + 1, value, 0)
+        return found
+
+    def offset(r, way):
+        if group != 8:
+            return lax.rem(mem + way * r + group, group)
+        code = pick(NEAR, r)
+        across = lax.rem(lax.div(mem, 4) + lax.div(code, 4), 2)
+        return across * 4 + lax.rem(lax.rem(mem, 4) + way * lax.rem(code, 4) + 4, 4)
+
     def member(r):
-        return lax.rem(mem + r, group)
+        return offset(r, 1)
 
     def far(r):
-        return lax.rem(grp + r, groups)
+        return lax.rem(grp + (pick(FAR, r) if groups == 8 else r), groups)
 
     def sweep(body, many):
         def turn(i, carry):
@@ -89,11 +104,11 @@
 
     def x_copy(i):
         band = pl.ds(i * BAND, BAND)
-        return pltpu.make_async_copy(x_hbm.at[band], xb.at[band], x_sem.at[i])
+        return pltpu.make_async_copy(x_hbm.at[band], xb.at[band], x_sem)
 
     def g_copy(i):
         band = pl.ds(i * BAND, BAND)
-        return pltpu.make_async_copy(gate_hbm.at[band], gb.at[band], g_sem.at[i])
+        return pltpu.make_async_copy(gate_hbm.at[band], gb.at[band], g_sem)
 
     for i in range(bands):
         x_copy(i).start()
@@ -113,7 +128,34 @@
 
     for i in range(bands):
         g_copy(i).start()
-    for copy in loads:
+
+    pl.semaphore_wait(barrier, 4 + (group - 1))
+    edge = 8
+    halo = [
+        pltpu.make_async_remote_copy(
+            src_ref=x_hbm.at[pl.ds(rows - edge, edge)], dst_ref=prev_v,
+            send_sem=h_send.at[0], recv_sem=h_recv.at[0],
+            device_id={"seq": after}, device_id_type=MESH,
+        ),
+        pltpu.make_async_remote_copy(
+            src_ref=x_hbm.at[pl.ds(0, edge)], dst_ref=next_v,
+            send_sem=h_send.at[1], recv_sem=h_recv.at[1],
+            device_id={"seq": before}, device_id_type=MESH,
+        ),
+    ]
+    for copy in halo:
+        copy.start()
+    rounds = groups // 2 - 1
+
+    def relay(k):
+        if 0 < k <= rounds:
+            pl.semaphore_wait(ready.at[k - 1], 2)
+        if k < rounds:
+            for peer in beside:
+                signal(ready.at[k], peer)
+
+    relay(0)
+    for copy in loads[:5]:
         copy.wait()
 
     first_t = lax.broadcasted_iota(jnp.int32, (rows, rows), 0)
@@ -159,44 +201,15 @@
         axis=1,
     )
 
-    for i in range(bands):
-        x_copy(i).wait()
-    pl.semaphore_wait(barrier, 4 + (group - 1))
-    rounds = groups // 2 - 1
-
-    def relay(k):
-        if 0 < k <= rounds:
-            pl.semaphore_wait(ready.at[k - 1], 2)
-        if k < rounds:
-            for peer in beside:
-                signal(ready.at[k], peer)
-
-    relay(0)
-    edge = 8
-    halo = [
-        pltpu.make_async_remote_copy(
-            src_ref=xb.at[pl.ds(rows - edge, edge)], dst_ref=prev_v,
-            send_sem=h_send.at[0], recv_sem=h_recv.at[0],
-            device_id={"seq": after}, device_id_type=MESH,
-        ),
-        pltpu.make_async_remote_copy(
-            src_ref=xb.at[pl.ds(0, edge)], dst_ref=next_v,
-            send_sem=h_send.at[1], recv_sem=h_recv.at[1],
-            device_id={"seq": before}, device_id_type=MESH,
-        ),
-    ]
-    for copy in halo:
-        copy.start()
-
     def near_copy(src, dst, ss, rs, r):
         return pltpu.make_async_remote_copy(
-            src_ref=src, dst_ref=dst, send_sem=ss.at[r - 1], recv_sem=rs.at[r - 1],
+            src_ref=src, dst_ref=dst, send_sem=ss, recv_sem=rs,
             device_id={"seq": base + member(r)}, device_id_type=MESH,
         )
 
     def far_copy(src, dst, ss, rs, r):
         return pltpu.make_async_remote_copy(
-            src_ref=src, dst_ref=dst, send_sem=ss.at[r - 1], recv_sem=rs.at[r - 1],
+            src_ref=src, dst_ref=dst, send_sem=ss, recv_sem=rs,
             device_id={"seq": far(r) * group + mem}, device_id_type=MESH,
         )
 
@@ -214,7 +227,14 @@
         return far_copy(send2.at[ahead], recv2.at[grp], c2_send, c2_recv, r)
 
     def c3(r):
-        return near_copy(send3.at[member(r)], recv3.at[mem], c3_send, c3_recv, r)
+        return near_copy(send3.at[member(r)], recv3.at[mem], c3_send, c3_recv.at[r - 1], r)
+
+    near_all, far_all = pl.ds(0, group - 1), pl.ds(0, groups - 1)
+    t1_all = near_copy(tots_v.at[near_all], tots_v.at[near_all], t1_send, t1_recv, 1)
+    t2_all = far_copy(totr_v.at[far_all], totr_v.at[far_all], t2_send, t2_recv, 1)
+    c1_all = near_copy(send1.at[near_all], recv1.at[near_all], c1_send, c1_recv, 1)
+    c2_all = far_copy(recv2.at[far_all], recv2.at[far_all], c2_send, c2_recv, 1)
+    c3_all = near_copy(send3.at[near_all], recv3.at[near_all], c3_send, c3_recv.at[0], 1)
 
     def loop(first, last, action):
         def body(r, carry):
@@ -226,20 +246,17 @@
     loop(1, group, lambda r: t1(r).start())
     tots_v[mem] = tot_v[...]
 
-    for i in range(bands):
-        g_copy(i).wait()
-
-    def outside(j):
-        wide = dot(lhs[...], spreader(j, heads, 2 * heads))
-        gate = silu(gb[:, lanes(j)].astype(F32))
-        sg[j] = gate
-        ef[j] = wide[:rows] * gate
-        er[j] = wide[rows : 2 * rows] * gate
-        gw[0, j] = wide[2 * rows : 3 * rows]
-        gw[1, j] = wide[3 * rows : 4 * rows]
-        ext[j] = wide[4 * rows : 4 * rows + 8]
-
-    sweep(outside, 3)
+    def growth(j):
+        wide = dot(lhs[pl.ds(2 * rows, 2 * rows + 16), :], spreader(j, heads, 2 * heads))
+        gw[0, j] = wide[:rows]
+        gw[1, j] = wide[rows : 2 * rows]
+        ext[j] = wide[2 * rows : 2 * rows + 8]
+
+    sweep(growth, 3)
+    relay(1)
+    for copy in loads[5:]:
+        copy.wait()
+    pltpu.make_async_copy(x_hbm, xb, x_sem).wait()
     for copy in halo:
         copy.wait()
 
@@ -283,27 +300,32 @@
 
     loop(1, group, ends)
     finish(mem, recv1)
-    relay(1)
-
-    loop(1, group, lambda r: t1(r).wait())
+    relay(2)
+
+    t1_all.wait()
     product = tots_v[0]
     for m in range(1, group):
         product = product * tots_v[m]
     totg_v[...] = product
     totr_v[grp] = product
+    pltpu.make_async_copy(gate_hbm, gb, g_sem).wait()
 
     def inner(j):
+        wide = dot(lhs[pl.ds(0, 2 * rows), :], spreader(j, heads, 2 * heads))
+        gate = silu(gb[:, lanes(j)].astype(F32))
+        far_f, far_r = wide[:rows] * gate, wide[rows:] * gate
+        ef[j] = far_f
+        er[j] = far_r
         direct = (
             ext[j, pl.ds(2, 1), :] * cf[j].astype(F32) + ext[j, pl.ds(3, 1), :] * cr[j].astype(F32)
         )
-        u[j] = (
-            direct * sg[j] + ef[j] * dot(mf[...], gf[j]) + er[j] * dot(mr[...], gr[j])
-        )
-
-    sweep(inner, 4)
-    relay(2)
-
-    loop(1, group, lambda r: c1(r).wait_recv())
+        u[j] = direct * gate + far_f * dot(mf[...], gf[j]) + far_r * dot(mr[...], gr[j])
+
+    sweep(inner, 3)
+    relay(3)
+    loop(1, groups, lambda r: t2(r).start())
+
+    c1_all.wait_recv()
 
     def spread(values, b):
         flat = values[...].reshape(-1, LANES)
@@ -326,13 +348,11 @@
             run_r = run_r * near_t[b][8 * k + 1 : 8 * k + 2] + part(recv1, k, b, 1)
         send2[0, b] = run_f.astype(BF16)
         send2[1, b] = run_r.astype(BF16)
-    relay(3)
-    loop(1, groups, lambda r: t2(r).start())
     loop(1, groups, lambda r: c2(r).start())
-    loop(1, groups, lambda r: t2(r).wait())
+    t2_all.wait()
     far_t = [spread(totr_v, b) for b in range(per)]
     recv2[grp] = send2[0]
-    loop(1, groups, lambda r: c2(r).wait_recv())
+    c2_all.wait_recv()
 
     for b in range(per):
         run_f = jnp.zeros((states, LANES), F32)
@@ -369,12 +389,12 @@
 
     def arrived(r):
         c3(r).wait_recv()
-        outer(lax.rem(mem + group - r, group))
+        outer(offset(r, -1))
 
     loop(1, group, arrived)
-    loop(1, group, lambda r: c1(r).wait_send())
-    loop(1, groups, lambda r: c2(r).wait_send())
-    loop(1, group, lambda r: c3(r).wait_send())
+    c1_all.wait_send()
+    c2_all.wait_send()
+    c3_all.wait_send()
 
 
 def finale(u, sumsq, gain_hbm, out_hbm, ob, gain_v, o_sem, s_sem):
@@ -387,7 +407,7 @@
 
     def o_copy(i):
         band = pl.ds(i * BAND, BAND)
-        return pltpu.make_async_copy(ob.at[band], out_hbm.at[band], o_sem.at[i])
+        return pltpu.make_async_copy(ob.at[band], out_hbm.at[band], o_sem)
 
     for i in range(rows // BAND):
         part = slice(i * BAND, (i + 1) * BAND)
@@ -395,8 +415,7 @@
             lanes = slice(j * LANES, (j + 1) * LANES)
             ob[part, lanes] = (u[j, part] * scale[part] * gain_v[:, lanes]).astype(BF16)
         o_copy(i).start()
-    for i in range(rows // BAND):
-        o_copy(i).wait()
+    pltpu.make_async_copy(ob, out_hbm, o_sem).wait()
 
 
 def solution(mesh, group=GROUP):
@@ -422,7 +441,6 @@
             wide16,
             wide16,
             wide16,
-            wide32,
             wide32,
             wide32,
             vm((2, blocks, rows, LANES), F32),
@@ -451,15 +469,14 @@
             vm((groups, per, states, LANES), BF16),
             vm((group, per, 2 * states, LANES), BF16),
             vm((group, per, 2 * states, LANES), BF16),
-            dma((rows // BAND,)),
-            dma((rows // BAND,)),
-            dma((8,)),
+            dma,
+            dma,
+            dma((7,)),
             pltpu.SemaphoreType.REGULAR((max(1, groups // 2 - 1),)),
             dma((2,)),
             dma((2,)),
         ]
-        near, far = dma((group - 1,)), dma((groups - 1,))
-        scratch += [near, near, far, far, near, near, far, far, near, near]
+        scratch += [dma] * 9 + [dma((group - 1,))]
         vmem = pl.BlockSpec(memory_space=pltpu.VMEM)
         hbm = pl.BlockSpec(memory_space=pl.ANY)
         gated, sumsq = pl.pallas_call(
@@ -489,7 +506,7 @@
             in_specs=[vmem, vmem, hbm],
             out_specs=hbm,
             scratch_shapes=[
-                vm((rows, width), BF16), vm((1, width), F32), dma((rows // BAND,)), dma
+                vm((rows, width), BF16), vm((1, width), F32), dma, dma
             ],
             compiler_params=pltpu.CompilerParams(vmem_limit_bytes=16 * 2**20),
             name="finale",

time: 39.9 us -> 37.8 us (0.947)
  Pallas kernels: 39.7 us -> 37.6 us
    pallas_call x1, Pallas kernels: 38.7 us -> 36.6 us  [local(): pl.pallas_call(functools.partial(kernel, n, group, heads, taps), out_shap...]
where the time goes in v4:
time: 37.8 us; the launch traced here: 37.6 us
  Pallas kernels  37.6 us (99%)
    pallas_call x1, Pallas kernels, local(): pl.pallas_call(functools.partial(kernel, n, group, heads, taps), out_shap...  36.6 us
    pallas_call x1, Pallas kernels, local(): pl.pallas_call(finale, out_shape=jax.ShapeDtypeStruct((rows, width), BF16...  1.04 us

profile of v4, /device:TPU:24, one launch (start us, length us, event | category | flops | bytes accessed | tf_op | source)
XLA Modules:
  0.0 37.6 jit_solution(3910617040484572283)
XLA Ops:
  0.0 0.0 copy-start
  0.0 36.6 %mixer.1 = (f32[24,128,128]{2,1,0:T(8,128)S(1)}, f32[128,128]{1,0:T(8,128)S(1)}) custom-call(bf16[128,3072]{1,0:T(8,128)(2,1)} %x_hbm.1, bf16[128,3072]{1,0:T(8,128)(2,1)} %gate_hbm.1, bf16[64,128]{1,0:T(8,128)(2,1)} %bitcast.5, bf16[96,128]{1,0:T(8,128)(2,1)} %bitcast.4, f32[2,4,3072]{2,1,0:T(4,128)} %cw_hbm.1, f32[2,3072]{1,0:T(2,128)} %cb_hbm.1, ...), custom_call_target="tpu_custom_call" | custom-call | tf_op jit(solution)/shard_map/mixer/pallas_call | solution.py:482
  36.6 0.0 copy-done
  36.6 1.0 %finale.1 = bf16[128,3072]{1,0:T(8,128)(2,1)} custom-call(f32[24,128,128]{2,1,0:T(8,128)S(1)} %get-tuple-element.7.u, f32[128,128]{1,0:T(8,128)S(1)} %get-tuple-element.8.sumsq, f32[1,3072]{1,0:T(1,128)S(1)} %bitcast.3), custom_call_target="tpu_custom_call" | custom-call | tf_op jit(solution)/shard_map/finale/pallas_call | solution.py:503
Async XLA Ops:
  0.0 36.6 %copy-start = (f32[3072]{0:T(1024)S(1)}, f32[3072]{0:T(1024)}, u32[]{:S(2)}) copy-start(f32[3072]{0:T(1024)} %param.19) | copy-start | bytes 36868

commit v5 on v4

--- a/solution.py
+++ b/solution.py
@@ -195,8 +195,8 @@
     lhs[...] = split(jnp.concatenate(decay + grow + total + skips + [zeros], axis=0))
     tot_v[...] = jnp.concatenate(
         [
-            jnp.concatenate(total + [jnp.zeros((6, heads), F32)], axis=0),
-            jnp.zeros((8, LANES - heads), F32),
+            jnp.concatenate(total, axis=0),
+            jnp.zeros((2, LANES - heads), F32),
         ],
         axis=1,
     )
@@ -222,19 +222,31 @@
     def c1(r):
         return near_copy(send1.at[member(r)], recv1.at[mem], c1_send, c1_recv, r)
 
-    def c2(r):
+    def c2(r, b):
         ahead = jnp.where(far(r) > grp, 0, 1)
-        return far_copy(send2.at[ahead], recv2.at[grp], c2_send, c2_recv, r)
-
-    def c3(r):
-        return near_copy(send3.at[member(r)], recv3.at[mem], c3_send, c3_recv.at[r - 1], r)
+        return far_copy(
+            send2.at[ahead, b], recv2.at[b, grp], c2_send.at[b], c2_recv.at[b], r
+        )
+
+    def c3(r, b):
+        return near_copy(
+            send3.at[b, member(r)], recv3.at[b, mem], c3_send.at[b], c3_recv.at[b], r
+        )
 
     near_all, far_all = pl.ds(0, group - 1), pl.ds(0, groups - 1)
     t1_all = near_copy(tots_v.at[near_all], tots_v.at[near_all], t1_send, t1_recv, 1)
     t2_all = far_copy(totr_v.at[far_all], totr_v.at[far_all], t2_send, t2_recv, 1)
     c1_all = near_copy(send1.at[near_all], recv1.at[near_all], c1_send, c1_recv, 1)
-    c2_all = far_copy(recv2.at[far_all], recv2.at[far_all], c2_send, c2_recv, 1)
-    c3_all = near_copy(send3.at[near_all], recv3.at[near_all], c3_send, c3_recv.at[0], 1)
+
+    def c2_all(b):
+        whole = recv2.at[b, far_all]
+        return far_copy(whole, whole, c2_send.at[b], c2_recv.at[b], 1)
+
+    def c3_all(b):
+        return near_copy(
+            send3.at[b, near_all], recv3.at[b, near_all], c3_send.at[b], c3_recv.at[b], 1
+        )
+
 
     def loop(first, last, action):
         def body(r, carry):
@@ -343,58 +355,62 @@
         run_f = jnp.zeros((states, LANES), F32)
         run_r = jnp.zeros((states, LANES), F32)
         for m in range(group):
-            run_f = run_f * near_t[b][8 * m : 8 * m + 1] + part(recv1, m, b, 0)
+            run_f = run_f * near_t[b][2 * m : 2 * m + 1] + part(recv1, m, b, 0)
             k = group - 1 - m
-            run_r = run_r * near_t[b][8 * k + 1 : 8 * k + 2] + part(recv1, k, b, 1)
+            run_r = run_r * near_t[b][2 * k + 1 : 2 * k + 2] + part(recv1, k, b, 1)
         send2[0, b] = run_f.astype(BF16)
         send2[1, b] = run_r.astype(BF16)
-    loop(1, groups, lambda r: c2(r).start())
+        loop(1, groups, lambda r: c2(r, b).start())
     t2_all.wait()
     far_t = [spread(totr_v, b) for b in range(per)]
-    recv2[grp] = send2[0]
-    c2_all.wait_recv()
-
     for b in range(per):
+        recv2[b, grp] = send2[0, b]
+
+    for b in range(per):
+        c2_all(b).wait_recv()
         run_f = jnp.zeros((states, LANES), F32)
         run_r = jnp.zeros((states, LANES), F32)
         for g in range(groups):
-            new = run_f * far_t[b][8 * g : 8 * g + 1] + recv2[g, b].astype(F32)
+            new = run_f * far_t[b][2 * g : 2 * g + 1] + recv2[b, g].astype(F32)
             run_f = jnp.where(g < grp, new, run_f)
             k = groups - 1 - g
-            new = run_r * far_t[b][8 * k + 1 : 8 * k + 2] + recv2[k, b].astype(F32)
+            new = run_r * far_t[b][2 * k + 1 : 2 * k + 2] + recv2[b, k].astype(F32)
             run_r = jnp.where(k > grp, new, run_r)
         for m in range(group):
-            send3[m, b, pl.ds(0, states), :] = run_f.astype(BF16)
-            run_f = run_f * near_t[b][8 * m : 8 * m + 1] + part(recv1, m, b, 0)
+            send3[b, m, pl.ds(0, states), :] = run_f.astype(BF16)
+            run_f = run_f * near_t[b][2 * m : 2 * m + 1] + part(recv1, m, b, 0)
             k = group - 1 - m
-            send3[k, b, pl.ds(states, states), :] = run_r.astype(BF16)
-            run_r = run_r * near_t[b][8 * k + 1 : 8 * k + 2] + part(recv1, k, b, 1)
-    loop(1, group, lambda r: c3(r).start())
-    recv3[mem] = send3[mem]
+            send3[b, k, pl.ds(states, states), :] = run_r.astype(BF16)
+            run_r = run_r * near_t[b][2 * k + 1 : 2 * k + 2] + part(recv1, k, b, 1)
+        loop(1, group, lambda r: c3(r, b).start())
+        recv3[b, mem] = send3[b, mem]
 
     sumsq[...] = jnp.zeros_like(sumsq)
-
-    def outer(owner):
-        for b in range(per):
-            j = owner * per + b
-            gated = (
-                u[j]
-                + ef[j] * dot(cm[0], recv3[owner, b, pl.ds(0, states), :])
-                + er[j] * dot(cm[1], recv3[owner, b, pl.ds(states, states), :])
-            )
-            u[j] = gated
-            sumsq[...] += gated * gated
-
-    outer(mem)
-
-    def arrived(r):
-        c3(r).wait_recv()
-        outer(offset(r, -1))
-
-    loop(1, group, arrived)
+    many = min(4, group)
+    for b in range(per):
+        c3_all(b).wait_recv()
+
+        def outer(i, carry):
+            squares = jnp.zeros((rows, LANES), F32)
+            for q in range(many):
+                owner = i * many + q
+                j = owner * per + b
+                gated = (
+                    u[j]
+                    + ef[j] * dot(cm[0], recv3[b, owner, pl.ds(0, states), :])
+                    + er[j] * dot(cm[1], recv3[b, owner, pl.ds(states, states), :])
+                )
+                u[j] = gated
+                squares = squares + gated * gated
+            sumsq[...] += squares
+            return carry
+
+        lax.fori_loop(0, group // many, outer, 0)
+
     c1_all.wait_send()
-    c2_all.wait_send()
-    c3_all.wait_send()
+    for b in range(per):
+        c2_all(b).wait_send()
+        c3_all(b).wait_send()
 
 
 def finale(u, sumsq, gain_hbm, out_hbm, ob, gain_v, o_sem, s_sem):
@@ -459,16 +475,16 @@
             vm((2, rows, states), BF16),
             vm((8, width), BF16),
             vm((8, width), BF16),
-            vm((8, LANES), F32),
-            vm((group, 8, LANES), F32),
-            vm((8, LANES), F32),
-            vm((groups, 8, LANES), F32),
+            vm((2, LANES), F32),
+            vm((group, 2, LANES), F32),
+            vm((2, LANES), F32),
+            vm((groups, 2, LANES), F32),
             vm((group, per, 2 * states, LANES), BF16),
             vm((group, per, 2 * states, LANES), BF16),
             vm((2, per, states, LANES), BF16),
-            vm((groups, per, states, LANES), BF16),
-            vm((group, per, 2 * states, LANES), BF16),
-            vm((group, per, 2 * states, LANES), BF16),
+            vm((per, groups, states, LANES), BF16),
+            vm((per, group, 2 * states, LANES), BF16),
+            vm((per, group, 2 * states, LANES), BF16),
             dma,
             dma,
             dma((7,)),
@@ -476,7 +492,7 @@
             dma((2,)),
             dma((2,)),
         ]
-        scratch += [dma] * 9 + [dma((group - 1,))]
+        scratch += [dma] * 6 + [dma((per,))] * 4
         vmem = pl.BlockSpec(memory_space=pltpu.VMEM)
         hbm = pl.BlockSpec(memory_space=pl.ANY)
         gated, sumsq = pl.pallas_call(

time: 37.8 us -> 37.3 us (0.987)
  Pallas kernels: 37.6 us -> 37.1 us
    pallas_call x1, Pallas kernels: 36.6 us -> 36.1 us  [local(): pl.pallas_call(functools.partial(kernel, n, group, heads, taps), out_shap...]
where the time goes in v5:
time: 37.3 us; the launch traced here: 37.2 us
  Pallas kernels  37.1 us (99%)
    pallas_call x1, Pallas kernels, local(): pl.pallas_call(functools.partial(kernel, n, group, heads, taps), out_shap...  36.1 us
    pallas_call x1, Pallas kernels, local(): pl.pallas_call(finale, out_shape=jax.ShapeDtypeStruct((rows, width), BF16...  1.04 us

profile of v5, /device:TPU:24, one launch (start us, length us, event | category | flops | bytes accessed | tf_op | source)
XLA Modules:
  0.0 37.2 jit_solution(1622142613171452735)
XLA Ops:
  0.0 0.0 copy-start
  0.0 36.1 %mixer.1 = (f32[24,128,128]{2,1,0:T(8,128)S(1)}, f32[128,128]{1,0:T(8,128)S(1)}) custom-call(bf16[128,3072]{1,0:T(8,128)(2,1)} %x_hbm.1, bf16[128,3072]{1,0:T(8,128)(2,1)} %gate_hbm.1, bf16[64,128]{1,0:T(8,128)(2,1)} %bitcast.5, bf16[96,128]{1,0:T(8,128)(2,1)} %bitcast.4, f32[2,4,3072]{2,1,0:T(4,128)} %cw_hbm.1, f32[2,3072]{1,0:T(2,128)} %cb_hbm.1, ...), custom_call_target="tpu_custom_call" | custom-call | tf_op jit(solution)/shard_map/mixer/pallas_call | solution.py:498
  36.1 0.0 copy-done
  36.1 1.0 %finale.1 = bf16[128,3072]{1,0:T(8,128)(2,1)} custom-call(f32[24,128,128]{2,1,0:T(8,128)S(1)} %get-tuple-element.7.u, f32[128,128]{1,0:T(8,128)S(1)} %get-tuple-element.8.sumsq, f32[1,3072]{1,0:T(1,128)S(1)} %bitcast.3), custom_call_target="tpu_custom_call" | custom-call | tf_op jit(solution)/shard_map/finale/pallas_call | solution.py:519
Async XLA Ops:
  0.0 36.1 %copy-start = (f32[3072]{0:T(1024)S(1)}, f32[3072]{0:T(1024)}, u32[]{:S(2)}) copy-start(f32[3072]{0:T(1024)} %param.19) | copy-start | bytes 36868

commit v6 on v5

--- a/solution.py
+++ b/solution.py
@@ -66,6 +66,8 @@
         return pl.ds(pl.multiple_of(j * LANES, LANES), LANES)
 
     def pick(table, r):
+        if isinstance(r, int):
+            return table[r - 1]
         found = 0
         for k, value in enumerate(table):
             found = found + jnp.where(r == k + 1, value, 0)
@@ -75,8 +77,9 @@
         if group != 8:
             return lax.rem(mem + way * r + group, group)
         code = pick(NEAR, r)
-        across = lax.rem(lax.div(mem, 4) + lax.div(code, 4), 2)
-        return across * 4 + lax.rem(lax.rem(mem, 4) + way * lax.rem(code, 4) + 4, 4)
+        high, low = (divmod(code, 4)) if isinstance(code, int) else (lax.div(code, 4), lax.rem(code, 4))
+        across = lax.rem(lax.div(mem, 4) + high, 2)
+        return across * 4 + lax.rem(lax.rem(mem, 4) + way * low + 4, 4)
 
     def member(r):
         return offset(r, 1)
@@ -155,12 +158,12 @@
                 signal(ready.at[k], peer)
 
     relay(0)
-    for copy in loads[:5]:
-        copy.wait()
-
     first_t = lax.broadcasted_iota(jnp.int32, (rows, rows), 0)
     second_t = lax.broadcasted_iota(jnp.int32, (rows, rows), 1)
     masks = (first_t >= second_t, first_t <= second_t)
+    for copy in loads[:5]:
+        copy.wait()
+
     lasts = (rows - 1, 0)
     raw = raw_v[...].astype(F32)
     params = jnp.concatenate(
@@ -255,7 +258,8 @@
 
         lax.fori_loop(first, last, body, 0)
 
-    loop(1, group, lambda r: t1(r).start())
+    for r in range(1, group):
+        t1(r).start()
     tots_v[mem] = tot_v[...]
 
     def growth(j):
@@ -264,7 +268,7 @@
         gw[1, j] = wide[rows : 2 * rows]
         ext[j] = wide[2 * rows : 2 * rows + 8]
 
-    sweep(growth, 3)
+    sweep(growth, 12)
     relay(1)
     for copy in loads[5:]:
         copy.wait()
@@ -333,9 +337,10 @@
         )
         u[j] = direct * gate + far_f * dot(mf[...], gf[j]) + far_r * dot(mr[...], gr[j])
 
-    sweep(inner, 3)
+    sweep(inner, 4)
     relay(3)
-    loop(1, groups, lambda r: t2(r).start())
+    for r in range(1, groups):
+        t2(r).start()
 
     c1_all.wait_recv()
 
@@ -360,7 +365,8 @@
             run_r = run_r * near_t[b][2 * k + 1 : 2 * k + 2] + part(recv1, k, b, 1)
         send2[0, b] = run_f.astype(BF16)
         send2[1, b] = run_r.astype(BF16)
-        loop(1, groups, lambda r: c2(r, b).start())
+        for r in range(1, groups):
+            c2(r, b).start()
     t2_all.wait()
     far_t = [spread(totr_v, b) for b in range(per)]
     for b in range(per):
@@ -382,7 +388,8 @@
             k = group - 1 - m
             send3[b, k, pl.ds(states, states), :] = run_r.astype(BF16)
             run_r = run_r * near_t[b][2 * k + 1 : 2 * k + 2] + part(recv1, k, b, 1)
-        loop(1, group, lambda r: c3(r, b).start())
+        for r in range(1, group):
+            c3(r, b).start()
         recv3[b, mem] = send3[b, mem]
 
     sumsq[...] = jnp.zeros_like(sumsq)
@@ -413,24 +420,17 @@
         c3_all(b).wait_send()
 
 
-def finale(u, sumsq, gain_hbm, out_hbm, ob, gain_v, o_sem, s_sem):
+def finale(u, sumsq, gain, out_hbm, ob, o_sem):
     blocks, rows, _ = u.shape
-    load = pltpu.make_async_copy(gain_hbm, gain_v, s_sem)
-    load.start()
     mean = jnp.sum(sumsq[...], axis=1, keepdims=True) * (1.0 / (blocks * LANES))
     scale = lax.rsqrt(mean + 1e-05)
-    load.wait()
-
-    def o_copy(i):
-        band = pl.ds(i * BAND, BAND)
-        return pltpu.make_async_copy(ob.at[band], out_hbm.at[band], o_sem)
-
-    for i in range(rows // BAND):
-        part = slice(i * BAND, (i + 1) * BAND)
+    for i in range(rows // 16):
+        part = slice(i * 16, (i + 1) * 16)
         for j in range(blocks):
             lanes = slice(j * LANES, (j + 1) * LANES)
-            ob[part, lanes] = (u[j, part] * scale[part] * gain_v[:, lanes]).astype(BF16)
-        o_copy(i).start()
+            ob[part, lanes] = (u[j, part] * scale[part] * gain[:, lanes]).astype(BF16)
+        band = pl.ds(i * 16, 16)
+        pltpu.make_async_copy(ob.at[band], out_hbm.at[band], o_sem).start()
     pltpu.make_async_copy(ob, out_hbm, o_sem).wait()
 
 
@@ -519,11 +519,9 @@
         return pl.pallas_call(
             finale,
             out_shape=jax.ShapeDtypeStruct((rows, width), BF16),
-            in_specs=[vmem, vmem, hbm],
+            in_specs=[vmem, vmem, vmem],
             out_specs=hbm,
-            scratch_shapes=[
-                vm((rows, width), BF16), vm((1, width), F32), dma, dma
-            ],
+            scratch_shapes=[vm((rows, width), BF16), dma],
             compiler_params=pltpu.CompilerParams(vmem_limit_bytes=16 * 2**20),
             name="finale",
         )(gated, sumsq, gain.reshape(1, width))

time: 37.3 us -> 37.2 us (level)
  no operation moved by 1% of the time
where the time goes in v6:
time: 37.2 us; the launch traced here: 37 us
  Pallas kernels  37 us (99%)
    pallas_call x1, Pallas kernels, local(): pl.pallas_call(functools.partial(kernel, n, group, heads, taps), out_shap...  35.9 us
    pallas_call x1, Pallas kernels, local(): pl.pallas_call(finale, out_shape=jax.ShapeDtypeStruct((rows, width), BF16...  1.09 us

profile of v6, /device:TPU:24, one launch (start us, length us, event | category | flops | bytes accessed | tf_op | source)
XLA Modules:
  0.0 37.0 jit_solution(16807874694255182523)
XLA Ops:
  0.0 0.0 copy-start
  0.0 35.9 %mixer.1 = (f32[24,128,128]{2,1,0:T(8,128)S(1)}, f32[128,128]{1,0:T(8,128)S(1)}) custom-call(bf16[128,3072]{1,0:T(8,128)(2,1)} %x_hbm.1, bf16[128,3072]{1,0:T(8,128)(2,1)} %gate_hbm.1, bf16[64,128]{1,0:T(8,128)(2,1)} %bitcast.5, bf16[96,128]{1,0:T(8,128)(2,1)} %bitcast.4, f32[2,4,3072]{2,1,0:T(4,128)} %cw_hbm.1, f32[2,3072]{1,0:T(2,128)} %cb_hbm.1, ...), custom_call_target="tpu_custom_call" | custom-call | tf_op jit(solution)/shard_map/mixer/pallas_call | solution.py:498
  35.9 0.0 copy-done
  35.9 1.1 %finale.1 = bf16[128,3072]{1,0:T(8,128)(2,1)} custom-call(f32[24,128,128]{2,1,0:T(8,128)S(1)} %get-tuple-element.7.u, f32[128,128]{1,0:T(8,128)S(1)} %get-tuple-element.8.sumsq, f32[1,3072]{1,0:T(1,128)S(1)} %bitcast.3), custom_call_target="tpu_custom_call" | custom-call | tf_op jit(solution)/shard_map/finale/pallas_call | solution.py:519
Async XLA Ops:
  0.0 35.9 %copy-start = (f32[3072]{0:T(1024)S(1)}, f32[3072]{0:T(1024)}, u32[]{:S(2)}) copy-start(f32[3072]{0:T(1024)} %param.19) | copy-start | bytes 36868

commit v7 on v6

--- a/solution.py
+++ b/solution.py
@@ -16,6 +16,8 @@
 NEAR = (6, 5, 7, 2, 4, 1, 3)
 FAR = (4, 3, 5, 2, 6, 1, 7)
 BAND = 32
+EDGE = 16
+HALO = 4
 
 
 def split(v):
@@ -49,7 +51,7 @@
     lhs, mf, mr, bt, cm,
     prev_v, next_v, tot_v, tots_v, totg_v, totr_v,
     send1, recv1, send2, recv2, send3, recv3,
-    x_sem, g_sem, s_sem, ready, h_send, h_recv,
+    e_sem, x_sem, g_sem, s_sem, ready, h_send, h_recv,
     t1_send, t1_recv, t2_send, t2_recv, c1_send, c1_recv, c2_send, c2_recv, c3_send, c3_recv,
 ):
     rows = u.shape[1]
@@ -100,21 +102,20 @@
         (skip_hbm, skip_v), (cw_hbm, cw_v), (cb_hbm, cb_v),
     ]
     loads = [pltpu.make_async_copy(a, b, s_sem.at[i]) for i, (a, b) in enumerate(small)]
-    for copy in loads:
+    bands = rows // BAND
+
+    def x_copy(first, count, semaphore):
+        band = pl.ds(first, count)
+        return pltpu.make_async_copy(x_hbm.at[band], xb.at[band], semaphore)
+
+    borders = [x_copy(0, EDGE, e_sem.at[0]), x_copy(rows - EDGE, EDGE, e_sem.at[1])]
+    middle = x_copy(EDGE, rows - 2 * EDGE, x_sem)
+    for copy in borders + loads + [middle]:
         copy.start()
-
-    bands = rows // BAND
-
-    def x_copy(i):
-        band = pl.ds(i * BAND, BAND)
-        return pltpu.make_async_copy(x_hbm.at[band], xb.at[band], x_sem)
 
     def g_copy(i):
         band = pl.ds(i * BAND, BAND)
         return pltpu.make_async_copy(gate_hbm.at[band], gb.at[band], g_sem)
-
-    for i in range(bands):
-        x_copy(i).start()
 
     barrier = pltpu.get_barrier_semaphore()
     after = lax.rem(me + 1, n)
@@ -133,15 +134,16 @@
         g_copy(i).start()
 
     pl.semaphore_wait(barrier, 4 + (group - 1))
-    edge = 8
+    for copy in borders:
+        copy.wait()
     halo = [
         pltpu.make_async_remote_copy(
-            src_ref=x_hbm.at[pl.ds(rows - edge, edge)], dst_ref=prev_v,
+            src_ref=xb.at[pl.ds(rows - HALO, HALO)], dst_ref=prev_v,
             send_sem=h_send.at[0], recv_sem=h_recv.at[0],
             device_id={"seq": after}, device_id_type=MESH,
         ),
         pltpu.make_async_remote_copy(
-            src_ref=x_hbm.at[pl.ds(0, edge)], dst_ref=next_v,
+            src_ref=xb.at[pl.ds(0, HALO)], dst_ref=next_v,
             send_sem=h_send.at[1], recv_sem=h_recv.at[1],
             device_id={"seq": before}, device_id_type=MESH,
         ),
@@ -272,7 +274,7 @@
     relay(1)
     for copy in loads[5:]:
         copy.wait()
-    pltpu.make_async_copy(x_hbm, xb, x_sem).wait()
+    middle.wait()
     for copy in halo:
         copy.wait()
 
@@ -282,8 +284,8 @@
     def conv(owner):
         for b in range(per):
             j = owner * per + b
-            xs[j, pl.ds(0, 8), :] = prev_v[:, lanes(j)].astype(F32) * has_before
-            xs[j, pl.ds(8 + rows, 8), :] = next_v[:, lanes(j)].astype(F32) * has_after
+            xs[j, pl.ds(8 - HALO, HALO), :] = prev_v[:, lanes(j)].astype(F32) * has_before
+            xs[j, pl.ds(8 + rows, HALO), :] = next_v[:, lanes(j)].astype(F32) * has_after
             xs[j, pl.ds(8, rows), :] = xb[:, lanes(j)].astype(F32)
         for b in range(per):
             j = owner * per + b
@@ -473,8 +475,8 @@
             vm((rows, rows), BF16),
             vm((2, states, rows), BF16),
             vm((2, rows, states), BF16),
-            vm((8, width), BF16),
-            vm((8, width), BF16),
+            vm((HALO, width), BF16),
+            vm((HALO, width), BF16),
             vm((2, LANES), F32),
             vm((group, 2, LANES), F32),
             vm((2, LANES), F32),
@@ -485,6 +487,7 @@
             vm((per, groups, states, LANES), BF16),
             vm((per, group, 2 * states, LANES), BF16),
             vm((per, group, 2 * states, LANES), BF16),
+            dma((2,)),
             dma,
             dma,
             dma((7,)),

time: 37.2 us -> 36.7 us (0.987)
  Pallas kernels: 37 us -> 36.5 us
    pallas_call x1, Pallas kernels: 35.9 us -> 35.4 us  [local(): pl.pallas_call(functools.partial(kernel, n, group, heads, taps), out_shap...]
where the time goes in v7:
time: 36.7 us; the launch traced here: 36.6 us
  Pallas kernels  36.5 us (99%)
    pallas_call x1, Pallas kernels, local(): pl.pallas_call(functools.partial(kernel, n, group, heads, taps), out_shap...  35.4 us
    pallas_call x1, Pallas kernels, local(): pl.pallas_call(finale, out_shape=jax.ShapeDtypeStruct((rows, width), BF16...  1.09 us

profile of v7, /device:TPU:24, one launch (start us, length us, event | category | flops | bytes accessed | tf_op | source)
XLA Modules:
  0.0 36.6 jit_solution(9906201737741961686)
XLA Ops:
  0.0 0.0 copy-start
  0.0 35.4 %mixer.1 = (f32[24,128,128]{2,1,0:T(8,128)S(1)}, f32[128,128]{1,0:T(8,128)S(1)}) custom-call(bf16[128,3072]{1,0:T(8,128)(2,1)} %x_hbm.1, bf16[128,3072]{1,0:T(8,128)(2,1)} %gate_hbm.1, bf16[64,128]{1,0:T(8,128)(2,1)} %bitcast.5, bf16[96,128]{1,0:T(8,128)(2,1)} %bitcast.4, f32[2,4,3072]{2,1,0:T(4,128)} %cw_hbm.1, f32[2,3072]{1,0:T(2,128)} %cb_hbm.1, ...), custom_call_target="tpu_custom_call" | custom-call | tf_op jit(solution)/shard_map/mixer/pallas_call | solution.py:501
  35.5 0.0 copy-done
  35.5 1.1 %finale.1 = bf16[128,3072]{1,0:T(8,128)(2,1)} custom-call(f32[24,128,128]{2,1,0:T(8,128)S(1)} %get-tuple-element.7.u, f32[128,128]{1,0:T(8,128)S(1)} %get-tuple-element.8.sumsq, f32[1,3072]{1,0:T(1,128)S(1)} %bitcast.3), custom_call_target="tpu_custom_call" | custom-call | tf_op jit(solution)/shard_map/finale/pallas_call | solution.py:522
Async XLA Ops:
  0.0 35.5 %copy-start = (f32[3072]{0:T(1024)S(1)}, f32[3072]{0:T(1024)}, u32[]{:S(2)}) copy-start(f32[3072]{0:T(1024)} %param.19) | copy-start | bytes 36868

commit v8 on v7

--- a/solution.py
+++ b/solution.py
@@ -97,6 +97,19 @@
 
         lax.fori_loop(0, blocks // many, turn, 0)
 
+    barrier = pltpu.get_barrier_semaphore()
+    after = lax.rem(me + 1, n)
+    before = lax.rem(me + n - 1, n)
+    beside = (lax.rem(me + group, n), lax.rem(me + n - group, n))
+
+    def signal(semaphore, peer):
+        pl.semaphore_signal(semaphore, inc=1, device_id={"seq": peer}, device_id_type=MESH)
+
+    for peer in (after, before) + beside:
+        signal(barrier, peer)
+    for r in range(1, group):
+        signal(barrier, base + member(r))
+
     small = [
         (raw_hbm, raw_v), (sb_hbm, sb_v), (rate_hbm, rate_v), (proj_hbm, proj_v),
         (skip_hbm, skip_v), (cw_hbm, cw_v), (cb_hbm, cb_v),
@@ -116,19 +129,6 @@
     def g_copy(i):
         band = pl.ds(i * BAND, BAND)
         return pltpu.make_async_copy(gate_hbm.at[band], gb.at[band], g_sem)
-
-    barrier = pltpu.get_barrier_semaphore()
-    after = lax.rem(me + 1, n)
-    before = lax.rem(me + n - 1, n)
-    beside = (lax.rem(me + group, n), lax.rem(me + n - group, n))
-
-    def signal(semaphore, peer):
-        pl.semaphore_signal(semaphore, inc=1, device_id={"seq": peer}, device_id_type=MESH)
-
-    for peer in (after, before) + beside:
-        signal(barrier, peer)
-    for r in range(1, group):
-        signal(barrier, base + member(r))
 
     for i in range(bands):
         g_copy(i).start()
@@ -148,8 +148,24 @@
             device_id={"seq": before}, device_id_type=MESH,
         ),
     ]
-    for copy in halo:
-        copy.start()
+    not_last, not_first = me < n - 1, me > 0
+
+    @pl.when(not_last)
+    def _():
+        halo[0].start()
+
+    @pl.when(not_first)
+    def _():
+        halo[1].start()
+
+    @pl.when(me == 0)
+    def _():
+        prev_v[...] = jnp.zeros_like(prev_v)
+
+    @pl.when(me == n - 1)
+    def _():
+        next_v[...] = jnp.zeros_like(next_v)
+
     rounds = groups // 2 - 1
 
     def relay(k):
@@ -275,17 +291,22 @@
     for copy in loads[5:]:
         copy.wait()
     middle.wait()
-    for copy in halo:
-        copy.wait()
-
-    has_before = jnp.where(me > 0, 1.0, 0.0)
-    has_after = jnp.where(me < n - 1, 1.0, 0.0)
+
+    @pl.when(not_last)
+    def _():
+        halo[0].wait_send()
+        halo[1].wait_recv()
+
+    @pl.when(not_first)
+    def _():
+        halo[1].wait_send()
+        halo[0].wait_recv()
 
     def conv(owner):
         for b in range(per):
             j = owner * per + b
-            xs[j, pl.ds(8 - HALO, HALO), :] = prev_v[:, lanes(j)].astype(F32) * has_before
-            xs[j, pl.ds(8 + rows, HALO), :] = next_v[:, lanes(j)].astype(F32) * has_after
+            xs[j, pl.ds(8 - HALO, HALO), :] = prev_v[:, lanes(j)].astype(F32)
+            xs[j, pl.ds(8 + rows, HALO), :] = next_v[:, lanes(j)].astype(F32)
             xs[j, pl.ds(8, rows), :] = xb[:, lanes(j)].astype(F32)
         for b in range(per):
             j = owner * per + b
@@ -316,7 +337,10 @@
         conv(member(r + 1))
         c1(r).start()
 
-    loop(1, group, ends)
+    loop(1, group - 1, ends)
+    finish(member(group - 1), send1)
+    c1(group - 1).start()
+    conv(mem)
     finish(mem, recv1)
     relay(2)
 
@@ -395,7 +419,7 @@
         recv3[b, mem] = send3[b, mem]
 
     sumsq[...] = jnp.zeros_like(sumsq)
-    many = min(4, group)
+    many = min(8, group)
     for b in range(per):
         c3_all(b).wait_recv()
 

time: 36.7 us -> 36.6 us (level)
  no operation moved by 1% of the time
where the time goes in v8:
time: 36.6 us; the launch traced here: 36.4 us
  Pallas kernels  36.4 us (99%)
    pallas_call x1, Pallas kernels, local(): pl.pallas_call(functools.partial(kernel, n, group, heads, taps), out_shap...  35.3 us
    pallas_call x1, Pallas kernels, local(): pl.pallas_call(finale, out_shape=jax.ShapeDtypeStruct((rows, width), BF16...  1.09 us

profile of v8, /device:TPU:24, one launch (start us, length us, event | category | flops | bytes accessed | tf_op | source)
XLA Modules:
  0.0 36.4 jit_solution(9769180735757274385)
XLA Ops:
  0.0 0.0 copy-start
  0.0 35.3 %mixer.1 = (f32[24,128,128]{2,1,0:T(8,128)S(1)}, f32[128,128]{1,0:T(8,128)S(1)}) custom-call(bf16[128,3072]{1,0:T(8,128)(2,1)} %x_hbm.1, bf16[128,3072]{1,0:T(8,128)(2,1)} %gate_hbm.1, bf16[64,128]{1,0:T(8,128)(2,1)} %bitcast.5, bf16[96,128]{1,0:T(8,128)(2,1)} %bitcast.4, f32[2,4,3072]{2,1,0:T(4,128)} %cw_hbm.1, f32[2,3072]{1,0:T(2,128)} %cb_hbm.1, ...), custom_call_target="tpu_custom_call" | custom-call | tf_op jit(solution)/shard_map/mixer/pallas_call | solution.py:525
  35.3 0.0 copy-done
  35.3 1.1 %finale.1 = bf16[128,3072]{1,0:T(8,128)(2,1)} custom-call(f32[24,128,128]{2,1,0:T(8,128)S(1)} %get-tuple-element.7.u, f32[128,128]{1,0:T(8,128)S(1)} %get-tuple-element.8.sumsq, f32[1,3072]{1,0:T(1,128)S(1)} %bitcast.3), custom_call_target="tpu_custom_call" | custom-call | tf_op jit(solution)/shard_map/finale/pallas_call | solution.py:546
Async XLA Ops:
  0.0 35.3 %copy-start = (f32[3072]{0:T(1024)S(1)}, f32[3072]{0:T(1024)}, u32[]{:S(2)}) copy-start(f32[3072]{0:T(1024)} %param.19) | copy-start | bytes 36868

commit v9 on v7

--- a/solution.py
+++ b/solution.py
@@ -316,7 +316,10 @@
         conv(member(r + 1))
         c1(r).start()
 
-    loop(1, group, ends)
+    loop(1, group - 1, ends)
+    finish(member(group - 1), send1)
+    c1(group - 1).start()
+    conv(mem)
     finish(mem, recv1)
     relay(2)
 
@@ -395,7 +398,7 @@
         recv3[b, mem] = send3[b, mem]
 
     sumsq[...] = jnp.zeros_like(sumsq)
-    many = min(4, group)
+    many = min(8, group)
     for b in range(per):
         c3_all(b).wait_recv()
 

time: 36.7 us -> 36.6 us (level)
  no operation moved by 1% of the time
where the time goes in v9:
time: 36.6 us; the launch traced here: 36.4 us
  Pallas kernels  36.4 us (99%)
    pallas_call x1, Pallas kernels, local(): pl.pallas_call(functools.partial(kernel, n, group, heads, taps), out_shap...  35.3 us
    pallas_call x1, Pallas kernels, local(): pl.pallas_call(finale, out_shape=jax.ShapeDtypeStruct((rows, width), BF16...  1.09 us

profile of v9, /device:TPU:24, one launch (start us, length us, event | category | flops | bytes accessed | tf_op | source)
XLA Modules:
  0.0 36.4 jit_solution(11980178383795735135)
XLA Ops:
  0.0 0.0 copy-start
  0.0 35.3 %mixer.1 = (f32[24,128,128]{2,1,0:T(8,128)S(1)}, f32[128,128]{1,0:T(8,128)S(1)}) custom-call(bf16[128,3072]{1,0:T(8,128)(2,1)} %x_hbm.1, bf16[128,3072]{1,0:T(8,128)(2,1)} %gate_hbm.1, bf16[64,128]{1,0:T(8,128)(2,1)} %bitcast.5, bf16[96,128]{1,0:T(8,128)(2,1)} %bitcast.4, f32[2,4,3072]{2,1,0:T(4,128)} %cw_hbm.1, f32[2,3072]{1,0:T(2,128)} %cb_hbm.1, ...), custom_call_target="tpu_custom_call" | custom-call | tf_op jit(solution)/shard_map/mixer/pallas_call | solution.py:504
  35.3 0.0 copy-done
  35.3 1.1 %finale.1 = bf16[128,3072]{1,0:T(8,128)(2,1)} custom-call(f32[24,128,128]{2,1,0:T(8,128)S(1)} %get-tuple-element.7.u, f32[128,128]{1,0:T(8,128)S(1)} %get-tuple-element.8.sumsq, f32[1,3072]{1,0:T(1,128)S(1)} %bitcast.3), custom_call_target="tpu_custom_call" | custom-call | tf_op jit(solution)/shard_map/finale/pallas_call | solution.py:525
Async XLA Ops:
  0.0 35.3 %copy-start = (f32[3072]{0:T(1024)S(1)}, f32[3072]{0:T(1024)}, u32[]{:S(2)}) copy-start(f32[3072]{0:T(1024)} %param.19) | copy-start | bytes 36868
